TPU v7x, 256 devices: a whole 4x4x8 slice. The times are simulated.
256 devices in a mesh: trial: 4 (over x), rows: 8 (over z), cols: 8 (over y, core).
Axes of the slice: x: 4, y: 4, z: 8, core: 2. Of those that a mesh axis runs over, the one named last changes fastest.
Arguments:
- weight_query: bfloat16 [20480, 5120], P(('trial', 'rows'), 'cols'), parts along dimension 0, may hold values from -0.078125 to 0.078125
- low_query: bfloat16 [20480, 32], P(('trial', 'rows')), parts along dimension 0, may hold values from -0.078125 to 0.078125
- high_query: bfloat16 [128, 5120], P('trial', 'cols'), parts along dimension 0, may hold values from -1 to 1
- weight_key: bfloat16 [20480, 1024], P(('trial', 'rows'), 'cols'), parts along dimension 0, may hold values from -0.078125 to 0.078125
- low_key: bfloat16 [20480, 32], P(('trial', 'rows')), parts along dimension 0, may hold values from -0.078125 to 0.078125
- high_key: bfloat16 [128, 1024], P('trial', 'cols'), parts along dimension 0, may hold values from -1 to 1
- weight_value: bfloat16 [20480, 1024], P(('trial', 'rows'), 'cols'), parts along dimension 0, may hold values from -0.078125 to 0.078125
- low_value: bfloat16 [20480, 32], P(('trial', 'rows')), parts along dimension 0, may hold values from -0.078125 to 0.078125
- high_value: bfloat16 [128, 1024], P('trial', 'cols'), parts along dimension 0, may hold values from -1 to 1
- norm_train: float32 [20480], P(('trial', 'rows', 'cols')), parts along dimension 0, may hold values from 0.25 to 1.75
- norm_step: float32 [20480], P(('trial', 'rows', 'cols')), parts along dimension 0, may hold values from -0.3 to 0.3
Outputs:
- serve_query: bfloat16 [20480, 5120], P(('trial', 'cols')), parts along dimension 0
- serve_key: bfloat16 [4096, 5120], P(('trial', 'cols')), parts along dimension 0
- serve_value: bfloat16 [4096, 5120], P(('trial', 'cols')), parts along dimension 0
- serve_norm: bfloat16 [20480], P('trial'), parts along dimension 0
There are 4 independent parts, one for each index of `trial`. A program takes and returns all parts, laid end to end along the dimension named above; each array names one. Nothing has to cross between parts.
All inputs are finite; a program needn't handle non-finite values.
Results may differ from a plain program's by a relative error of at most 0.001.
Values may be sent and summed in bfloat16 or wider, within the bound.
A program may use at most 64 MiB of HBM per device.

v0:
```python
import jax
import jax.numpy as jnp
from jax import lax
from jax.sharding import PartitionSpec as P

mix_rate = 2.0


def in_one_piece(arrays, axis, dim, along):
    widths = [a.shape[along] for a in arrays]
    both = jnp.concatenate(arrays, axis=along)
    result = lax.all_gather(both, axis, axis=dim, tiled=True)
    return tuple(jnp.split(result, [sum(widths[:k]) for k in range(1, len(widths))], axis=along))


def joined_along(pieces, dim):
    pieces = jnp.moveaxis(pieces, 0, dim)
    dims = pieces.shape
    return pieces.reshape(*dims[:dim], dims[dim] * dims[dim + 1], *dims[dim + 2 :])


def from_everyone(shard, axis):
    copies = jnp.broadcast_to(shard, (lax.axis_size(axis), *shard.shape))
    return lax.all_to_all(copies, axis, split_axis=0, concat_axis=0, tiled=True)


def gathered_copies(shard, axis, dim):
    return joined_along(from_everyone(shard, axis), dim)


def local(
    weight_query,
    low_query,
    high_query,
    weight_key,
    low_key,
    high_key,
    weight_value,
    low_value,
    high_value,
    norm_train,
    norm_step,
):
    fresh_query = weight_query.astype(jnp.float32) + mix_rate * jnp.dot(
        low_query, high_query, preferred_element_type=jnp.float32
    )
    fresh_key = weight_key.astype(jnp.float32) + mix_rate * jnp.dot(
        low_key, high_key, preferred_element_type=jnp.float32
    )
    fresh_value = weight_value.astype(jnp.float32) + mix_rate * jnp.dot(
        low_value, high_value, preferred_element_type=jnp.float32
    )
    narrow_query, narrow_key, narrow_value = (
        fresh_query.astype(jnp.bfloat16),
        fresh_key.astype(jnp.bfloat16),
        fresh_value.astype(jnp.bfloat16),
    )
    serve_query, serve_key, serve_value = in_one_piece(
        (narrow_query, narrow_key, narrow_value), "rows", 0, 1
    )
    serve_query, serve_key, serve_value = (serve_query.T, serve_key.T, serve_value.T)
    serve_norm = gathered_copies((norm_train + norm_step).astype(jnp.bfloat16), ("rows", "cols"), 0)
    return (serve_query, serve_key, serve_value, serve_norm)


def solution(mesh):
    return jax.shard_map(
        local,
        mesh=mesh,
        in_specs=(
            P(("trial", "rows"), "cols"),
            P(("trial", "rows"), None),
            P("trial", "cols"),
            P(("trial", "rows"), "cols"),
            P(("trial", "rows"), None),
            P("trial", "cols"),
            P(("trial", "rows"), "cols"),
            P(("trial", "rows"), None),
            P("trial", "cols"),
            P(("trial", "rows", "cols")),
            P(("trial", "rows", "cols")),
        ),
        out_specs=(
            P(("trial", "cols"), None),
            P(("trial", "cols"), None),
            P(("trial", "cols"), None),
            P("trial"),
        ),
        check_vma=False,
    )
```

profile of v0, /device:TPU:24, one launch (start us, length us, event | category | flops | bytes accessed | tf_op | source)
XLA Modules:
  0.0 132.4 jit_solution(9697362623909140216)
XLA Ops:
  7.2 0.0 copy-start
  7.2 0.0 copy-start.1
  7.2 0.0 copy-start.2
  7.2 0.0 copy-start.5
  7.2 0.0 copy-start.3
  7.2 0.0 copy-start.6
  7.2 0.0 all-gather.2.cloned.1.call-start
  7.3 1.9 %copy.21 = bf16[640,640]{0,1:T(8,128)(2,1)S(1)} copy(bf16[640,640]{1,0:T(8,128)(2,1)} %param.11) | data formatting | bytes 1638400 | tf_op args[0]
  9.2 0.0 copy-done.1
  9.2 0.0 copy-start.4
  9.2 0.0 copy-start.7
  9.2 0.2 copy.22
  9.4 0.0 copy-done.2
  9.4 0.2 copy.23
  9.6 0.0 copy-done
  9.6 0.0 copy-done.5
  9.6 0.4 add_convert_fusion
  10.0 0.0 copy-done.3
  10.0 0.0 copy-done.6
  10.0 0.3 fusion.2
  10.3 0.0 copy-done.4
  10.3 0.0 copy-done.7
  10.3 0.3 fusion.3
  10.6 0.0 copy-start.8
  10.6 0.0 copy-start.9
  10.6 1.1 pad_maximum_fusion
  11.7 0.0 all-gather.2.cloned.1.call-update
  11.7 0.0 copy-done.8
  11.7 0.0 copy-done.9
  11.8 19.6 %all_to_all.6 = bf16[64,1,80]{2,1,0:T(2,128)(2,1)S(1)} all-to-all(bf16[64,1,80]{2,1,0:T(2,128)(2,1)S(1)} %broadcast_in_dim.3), channel_id=1, replica_groups=mesh['trial'=4,'rows'=8,'cols'=8] {'rows','cols'}, dimensions={0} | all-to-all | bytes 20480 | tf_op jit(solution)/shard_map/all_to_all | solution.py:24
  31.4 0.1 reduce
  31.5 0.7 reshape.16
  32.2 84.0 %all-gather.2.cloned.1.call-done = bf16[5120,896]{0,1:T(8,128)(2,1)} async-done(((bf16[640,896]{0,1:T(8,128)(2,1)}), bf16[5120,896]{0,1:T(8,128)(2,1)}) %all-gather.2.cloned.1.call-update) | async-done | bytes 9175056 | tf_op jit(solution)/shard_map/all_gather | solution.py:12
  116.2 3.4 %slice_bitcast_fusion.1 = (bf16[128,5120]{1,0:T(8,128)(2,1)}, bf16[128,5120]{1,0:T(8,128)(2,1)}) fusion(bf16[5120,896]{0,1:T(8,128)(2,1)} %all-gather.2.cloned.1.call-done), kind=kLoop, calls=%fused_computation.2 | loop fusion | bytes 5242880 | tf_op jit(solution)/shard_map/transpose | solution.py:61
  119.5 6.1 %slice_bitcast_fusion = bf16[640,5120]{1,0:T(8,128)(2,1)} fusion(bf16[5120,896]{0,1:T(8,128)(2,1)} %all-gather.2.cloned.1.call-done), kind=kLoop, calls=%fused_computation | loop fusion | bytes 13107200 | tf_op jit(solution)/shard_map/transpose | solution.py:61
  (2 shorter events, 0.0 us)
Async XLA Ops:
  7.2 2.4 %copy-start = (bf16[640,32]{0,1:T(8,128)(2,1)S(1)}, bf16[640,32]{0,1:T(8,128)(2,1)}, u32[]{:S(2)}) copy-start(bf16[640,32]{0,1:T(8,128)(2,1)} %param.12) | copy-start | bytes 122884
  7.2 2.0 %copy-start.1 = (bf16[640,128]{1,0:T(8,128)(2,1)S(1)}, bf16[640,128]{1,0:T(8,128)(2,1)}, u32[]{:S(2)}) copy-start(bf16[640,128]{1,0:T(8,128)(2,1)} %param.14) | copy-start | bytes 491524
  7.2 2.2 %copy-start.2 = (bf16[640,128]{1,0:T(8,128)(2,1)S(1)}, bf16[640,128]{1,0:T(8,128)(2,1)}, u32[]{:S(2)}) copy-start(bf16[640,128]{1,0:T(8,128)(2,1)} %param.17) | copy-start | bytes 491524
  7.2 2.4 %copy-start.5 = (bf16[32,640]{1,0:T(8,128)(2,1)S(1)}, bf16[32,640]{1,0:T(8,128)(2,1)}, u32[]{:S(2)}) copy-start(bf16[32,640]{1,0:T(8,128)(2,1)} %param.13) | copy-start | bytes 122884
  7.2 2.8 %copy-start.3 = (bf16[640,32]{0,1:T(8,128)(2,1)S(1)}, bf16[640,32]{0,1:T(8,128)(2,1)}, u32[]{:S(2)}) copy-start(bf16[640,32]{0,1:T(8,128)(2,1)} %param.15) | copy-start | bytes 122884
  7.2 2.8 %copy-start.6 = (bf16[32,128]{1,0:T(8,128)(2,1)S(1)}, bf16[32,128]{1,0:T(8,128)(2,1)}, u32[]{:S(2)}) copy-start(bf16[32,128]{1,0:T(8,128)(2,1)} %param.16) | copy-start | bytes 24580
  7.2 108.9 %all-gather.2.cloned.1.call-start = ((), (), s32[]{:S(2)}) async-start(), calls=%async_computation.1 | async-start | bytes 10321920 | tf_op jit(solution)/shard_map/all_gather | solution.py:12
  9.2 1.1 copy-start.4
  9.2 1.1 copy-start.7
  10.6 1.2 copy-start.8
  10.6 1.2 copy-start.9
Sparse Core Ops, SparseCore 0:
  11.8 104.2 all-gather.1
where the time goes:
time: 134 us; the launch traced here: 132 us
  waiting for transfers between devices  84 us (63%)
  blocking collectives  19.6 us (15%)
  between operations  14.2 us (11%)
  local copies, waits for them, and re-layouts  12.4 us (9%)
    all_gather x1, waiting for transfers between devices, in_one_piece(): result = lax.all_gather(both, axis, axis=dim, tiled=True)  84 us
    all_to_all x1, blocking collectives, from_everyone(): return lax.all_to_all(copies, axis, split_axis=0, concat_axis=0, tiled=True)  19.6 us
    transpose x2, local copies, waits for them, and re-layouts, local(): serve_query, serve_key, serve_value = (serve_query.T, serve_key.T, serve_...  9.44 us
  transfers between devices with their start and end apart: 1, of which 1 were waited for; matrix products, arithmetic and copies ran while one was open for 1% of the time, Pallas kernels for 0%

commit v1 on v0

v1 whole, which is shorter than its diff:
```python
import functools

import jax
import jax.numpy as jnp
from jax import lax
from jax.experimental import pallas as pl
from jax.experimental.pallas import tpu as pltpu
from jax.sharding import PartitionSpec as P

MESH = pl.DeviceIdType.MESH
MIX = 2.0
F32 = jnp.float32
BF16 = jnp.bfloat16

N = 8
ROWS = 640
COLS = (640, 128, 128)
WIDTH = sum(COLS)
PIECES = ((0, 128), (128, 128), (256, 128), (384, 64), (448, 64), (512, 128), (640, 128), (768, 128))
NP = len(PIECES)
HALF = NP // 2
RIGHT = [(h, p) for h in range(3) for p in range(NP)] + [(3, p) for p in range(HALF)]
LEFT = [(h, p) for h in range(3) for p in range(NP)] + [(3, p) for p in range(HALF, NP)]
ORDERS = (RIGHT, LEFT)
NS = len(RIGHT)
DEPTH = 4
PAD = 128


def exchange(
    wq, lq, hq, wk, lk, hk, wv, lv, hv, nt, ns,
    buf, gain,
    wq_v, wk_v, wv_v, lq_v, lk_v, lv_v, hq_v, hk_v, hv_v, nt_v, ns_v, gains,
    in_sem, send_sem, recv_sem, gsend, grecv, psend, precv,
):
    z = lax.axis_index("rows")
    c = lax.axis_index("cols")
    right, left = lax.rem(z + 1, N), lax.rem(z + N - 1, N)
    up, down = lax.rem(c + 2, N), lax.rem(c + N - 2, N)
    partner = c + 1 - 2 * lax.rem(c, 2)

    barrier = pltpu.get_barrier_semaphore()
    for who in ({"rows": right}, {"rows": left}, {"cols": up}, {"cols": down}, {"cols": partner}):
        pl.semaphore_signal(barrier, inc=1, device_id=who, device_id_type=MESH)

    loads = []

    def load(src, dst):
        copy = pltpu.make_async_copy(src, dst, in_sem.at[len(loads)])
        copy.start()
        loads.append(copy)
        return copy


    got_lq = load(lq, lq_v)
    got_hq = load(hq, hq_v)
    got_wq = [load(wq.at[:, pl.ds(i * 128, 128)], wq_v.at[i]) for i in range(5)]
    got_nt, got_ns = load(nt, nt_v), load(ns, ns_v)
    got_k = [load(wk, wk_v), load(lk, lk_v), load(hk, hk_v)]
    got_v = [load(wv, wv_v), load(lv, lv_v), load(hv, hv_v)]

    def merged(w, h, lt):
        wt = w.T.astype(F32)
        d = lax.dot_general(h, lt, (((0,), (0,)), ((), ())), preferred_element_type=F32)
        return (wt + MIX * d).astype(BF16)

    def compute(i):
        rows = pl.ds(i * 128, 128)
        if i == 0:
            got_lq.wait()
            got_hq.wait()
        if i < 5:
            got_wq[i].wait()
            buf[z, rows, :] = merged(wq_v[i], hq_v[:, i * 128 : (i + 1) * 128], lq_v[...])
        elif i == 5:
            for x in got_k:
                x.wait()
            buf[z, rows, :] = merged(wk_v[...], hk_v[...], lk_v[...])
        else:
            for x in got_v:
                x.wait()
            buf[z, rows, :] = merged(wv_v[...], hv_v[...], lv_v[...])

    hops = ((right, 1), (left, -1))

    def piece_copy(d, k):
        hop, p = ORDERS[d][k]
        to, sign = hops[d]
        src = lax.rem(z - sign * hop + N, N)
        first, height = PIECES[p]
        ref = buf.at[src, pl.ds(first, height), :]
        return pltpu.make_async_remote_copy(
            src_ref=ref, dst_ref=ref, send_sem=send_sem.at[d, k], recv_sem=recv_sem.at[d, k],
            device_id={"rows": to}, device_id_type=MESH,
        )

    def arrival(d, k):
        hop, p = ORDERS[d][k]
        to, sign = hops[d]
        src = lax.rem(z - sign * (hop + 1) + 2 * N, N)
        first, height = PIECES[p]
        ref = buf.at[src, pl.ds(first, height), :]
        return pltpu.make_async_remote_copy(
            src_ref=ref, dst_ref=ref, send_sem=send_sem.at[d, k], recv_sem=recv_sem.at[d, k],
            device_id={"rows": to}, device_id_type=MESH,
        )

    def gain_copy(d, hop):
        to, sign = hops[d]
        ref = gains.at[c, lax.rem(z - sign * hop + N, N)]
        return pltpu.make_async_remote_copy(
            src_ref=ref, dst_ref=ref, send_sem=gsend.at[d, hop], recv_sem=grecv.at[d, hop],
            device_id={"rows": to}, device_id_type=MESH,
        )

    def gain_arrival(d, hop):
        to, sign = hops[d]
        ref = gains.at[c, lax.rem(z - sign * (hop + 1) + 2 * N, N)]
        return pltpu.make_async_remote_copy(
            src_ref=ref, dst_ref=ref, send_sem=gsend.at[d, hop], recv_sem=grecv.at[d, hop],
            device_id={"rows": to}, device_id_type=MESH,
        )

    pair = c - lax.rem(c, 2)

    def partner_copy(col):
        ref = gains.at[col]
        return pltpu.make_async_remote_copy(
            src_ref=ref, dst_ref=ref, send_sem=psend.at[0], recv_sem=precv.at[0],
            device_id={"cols": partner}, device_id_type=MESH,
        )

    def pair_copy(hop, back):
        ref = gains.at[pl.ds(lax.rem(pair - 2 * (hop + back) + 2 * N, N), 2)]
        return pltpu.make_async_remote_copy(
            src_ref=ref, dst_ref=ref, send_sem=psend.at[1 + hop], recv_sem=precv.at[1 + hop],
            device_id={"cols": up}, device_id_type=MESH,
        )

    def norm_step(k):
        if k == 1:
            for d in range(2):
                gain_copy(d, 0).start()
        elif k in (5, 9, 13):
            hop = (k - 1) // 4
            for d in range(2):
                if hop < 4 - d:
                    gain_arrival(d, hop - 1).wait_recv()
                    gain_copy(d, hop).start()
        elif k == 17:
            gain_arrival(1, 2).wait_recv()
            gain_arrival(0, 3).wait_recv()
            partner_copy(c).start()
        elif k == 19:
            partner_copy(partner).wait_recv()
            pair_copy(0, 0).start()
        elif k in (21, 23):
            hop = (k - 19) // 2
            pair_copy(hop - 1, 1).wait_recv()
            pair_copy(hop, 0).start()
        elif k == 26:
            pair_copy(2, 1).wait_recv()
            lane = lax.broadcasted_iota(jnp.int32, (N, PAD), 1)
            rows = [jnp.zeros((N, PAD), F32) for _ in range(5)]
            for j in range(N):
                v = gains[j].reshape(N, PAD)
                row, off = divmod(80 * j, PAD)
                r = pltpu.roll(v, off, 1) if off else v
                rows[row] = jnp.where((lane >= off) & (lane < off + 80), r, rows[row])
                if off + 80 > PAD:
                    rows[row + 1] = jnp.where(lane < off + 80 - PAD, r, rows[row + 1])
            for j in range(5):
                gain[pl.ds(j, N, stride=5), :] = rows[j]

    compute(0)
    got_nt.wait()
    got_ns.wait()
    gains[c, z, 0:1, 0:80] = (nt_v[...] + ns_v[...]).reshape(1, 80)
    compute(1)
    pl.semaphore_wait(barrier, 5)
    done = 2
    for k in range(NS):
        norm_step(k)
        for d in range(2):
            hop, p = ORDERS[d][k]
            if hop:
                arrival(d, ORDERS[d].index((hop - 1, p))).wait_recv()
            if k >= DEPTH:
                piece_copy(d, k - DEPTH).wait_send()
            piece_copy(d, k).start()
        if k < NP and done < 7:
            compute(done)
            done += 1
    for d in range(2):
        for k in range(NS):
            hop, p = ORDERS[d][k]
            if (hop + 1, p) not in ORDERS[d]:
                arrival(d, k).wait_recv()
    for d in range(2):
        for k in range(NS - DEPTH, NS):
            piece_copy(d, k).wait_send()
        for hop in range(4 - d):
            gain_copy(d, hop).wait_send()
    partner_copy(c).wait_send()
    for hop in range(3):
        pair_copy(hop, 0).wait_send()


def deliver(buf, gain, q, k, v, g, sem):
    copies = []
    for r in range(N):
        at = pl.ds(r * ROWS, ROWS)
        first = 0
        for out, width in zip((q, k, v), COLS):
            copy = pltpu.make_async_copy(buf.at[r, pl.ds(first, width), :], out.at[:, at], sem.at[len(copies)])
            copy.start()
            copies.append(copy)
            first += width
    g[...] = gain[...].astype(BF16)
    for copy in copies:
        copy.wait()


def local(wq, lq, hq, wk, lk, hk, wv, lv, hv, nt, ns):
    hbm = pl.BlockSpec(memory_space=pltpu.HBM)
    vmem = pl.BlockSpec(memory_space=pltpu.VMEM)
    dma = pltpu.SemaphoreType.DMA
    buf, gain = pl.pallas_call(
        exchange,
        name="exchange",
        out_shape=(
            jax.ShapeDtypeStruct((N, WIDTH, ROWS), BF16),
            jax.ShapeDtypeStruct((40, PAD), F32),
        ),
        in_specs=[hbm] * 11,
        out_specs=(vmem, vmem),
        scratch_shapes=[
            pltpu.VMEM((5, ROWS, 128), BF16),
            pltpu.VMEM((ROWS, 128), BF16),
            pltpu.VMEM((ROWS, 128), BF16),
            pltpu.VMEM((32, ROWS), BF16),
            pltpu.VMEM((32, ROWS), BF16),
            pltpu.VMEM((32, ROWS), BF16),
            pltpu.VMEM((32, 640), BF16),
            pltpu.VMEM((32, 128), BF16),
            pltpu.VMEM((32, 128), BF16),
            pltpu.VMEM((80,), F32),
            pltpu.VMEM((80,), F32),
            pltpu.VMEM((N, N, 1, PAD), F32),
            dma((16,)),
            dma((2, NS)),
            dma((2, NS)),
            dma((2, 4)),
            dma((2, 4)),
            dma((4,)),
            dma((4,)),
        ],
        compiler_params=pltpu.CompilerParams(
            collective_id=0, has_side_effects=True, vmem_limit_bytes=24 << 20
        ),
    )(*(pltpu.with_memory_space_constraint(x, pltpu.HBM) for x in (wq, lq.T, hq, wk, lk.T, hk, wv, lv.T, hv, nt, ns)))
    q, k, v, g = pl.pallas_call(
        deliver,
        name="deliver",
        out_shape=(
            jax.ShapeDtypeStruct((COLS[0], N * ROWS), BF16),
            jax.ShapeDtypeStruct((COLS[1], N * ROWS), BF16),
            jax.ShapeDtypeStruct((COLS[2], N * ROWS), BF16),
            jax.ShapeDtypeStruct((40, PAD), BF16),
        ),
        in_specs=[vmem, vmem],
        out_specs=(hbm, hbm, hbm, vmem),
        scratch_shapes=[dma((24,))],
        compiler_params=pltpu.CompilerParams(vmem_limit_bytes=24 << 20),
    )(buf, gain)
    return q, k, v, g.reshape(N * ROWS)


def solution(mesh):
    return jax.shard_map(
        local,
        mesh=mesh,
        in_specs=(
            P(("trial", "rows"), "cols"),
            P(("trial", "rows"), None),
            P("trial", "cols"),
            P(("trial", "rows"), "cols"),
            P(("trial", "rows"), None),
            P("trial", "cols"),
            P(("trial", "rows"), "cols"),
            P(("trial", "rows"), None),
            P("trial", "cols"),
            P(("trial", "rows", "cols")),
            P(("trial", "rows", "cols")),
        ),
        out_specs=(
            P(("trial", "cols"), None),
            P(("trial", "cols"), None),
            P(("trial", "cols"), None),
            P("trial"),
        ),
        check_vma=False,
    )
```

time: 134 us -> 102 us (0.76)
  Pallas kernels: 0 us -> 100 us
  waiting for transfers between devices: 84 us -> 0 us
  blocking collectives: 19.6 us -> 0 us
  between operations: 14.2 us -> 0.64 us
  local copies, waits for them, and re-layouts: 12.4 us -> 0 us
    pallas_call x0 -> x2, Pallas kernels: none -> 100 us  [the longest x1 95.6 us: local(): pl.pallas_call(exchange, name='exchange', out_shape=(jax.ShapeDtypeStruct...]
    all_gather x1 -> x0, waiting for transfers between devices: 84 us -> none  [in_one_piece(): result = lax.all_gather(both, axis, axis=dim, tiled=True)]
    all_to_all x1 -> x0, blocking collectives: 19.6 us -> none  [from_everyone(): return lax.all_to_all(copies, axis, split_axis=0, concat_axis=0, tiled=True)]
    transpose x2 -> x0, local copies, waits for them, and re-layouts: 9.44 us -> none  [local(): serve_query, serve_key, serve_value = (serve_query.T, serve_key.T, serve_...]
    unnamed x23 -> x0, local copies, waits for them, and re-layouts: 2.28 us -> none
  transfers between devices with their start and end apart: 1 -> 0, of which waited for: 1 -> 0; matrix products, arithmetic and copies ran while one was open for 1% -> 0% of each run, Pallas kernels for 0% -> 0%
where the time goes in v1:
time: 102 us; the launch traced here: 101 us
  Pallas kernels  100 us (98%)
    pallas_call x1, Pallas kernels, local(): pl.pallas_call(exchange, name='exchange', out_shape=(jax.ShapeDtypeStruct...  95.6 us
    pallas_call x1, Pallas kernels, local(): pl.pallas_call(deliver, name='deliver', out_shape=(jax.ShapeDtypeStruct((...  4.31 us

profile of v1, /device:TPU:24, one launch (start us, length us, event | category | flops | bytes accessed | tf_op | source)
XLA Modules:
  0.0 100.6 jit_solution(5248137454775949778)
XLA Ops:
  0.6 95.6 %exchange.1 = (bf16[8,896,640]{2,1,0:T(8,128)(2,1)S(1)}, f32[40,128]{1,0:T(8,128)S(1)}) custom-call(bf16[640,640]{1,0:T(8,128)(2,1)} %wq.1, bf16[32,640]{1,0:T(8,128)(2,1)} %bitcast.4, bf16[32,640]{1,0:T(8,128)(2,1)} %hq.1, bf16[640,128]{1,0:T(8,128)(2,1)} %wk.1, bf16[32,640]{1,0:T(8,128)(2,1)} %bitcast.5, bf16[32,128]{1,0:T(8,128)(2,1)} %hk.1, ...), custom_call_target="tpu_custom_call" | custom-call | tf_op jit(solution)/shard_map/exchange/pallas_call | solution.py:228
  96.3 4.3 %deliver.1 = (bf16[640,5120]{1,0:T(8,128)(2,1)}, bf16[128,5120]{1,0:T(8,128)(2,1)}, bf16[128,5120]{1,0:T(8,128)(2,1)}, bf16[40,128]{1,0:T(8,128)(2,1)}) custom-call(bf16[8,896,640]{2,1,0:T(8,128)(2,1)S(1)} %get-tuple-element.10.buf, f32[40,128]{1,0:T(8,128)S(1)} %get-tuple-element.11.gain), custom_call_target="tpu_custom_call" | custom-call | tf_op jit(solution)/shard_map/deliver/pallas_call | solution.py:262

commit v2 on v0

v2 whole, which is shorter than its diff:
```python
import functools

import jax
import jax.numpy as jnp
from jax import lax
from jax.experimental import pallas as pl
from jax.experimental.pallas import tpu as pltpu
from jax.sharding import PartitionSpec as P

MESH = pl.DeviceIdType.MESH
MIX = 2.0
F32 = jnp.float32
BF16 = jnp.bfloat16

N = 8
ROWS = 640
COLS = (640, 128, 128)
WIDTH = sum(COLS)
PAD = 128
UNIT = 128
PIECES = ((0, 128), (128, 128), (256, 128), (384, 64), (448, 64), (512, 128), (640, 128), (768, 128))
NP = len(PIECES)
UNIT_OF = (0, 1, 2, 3, 3, 4, 5, 6)
ORDERS = tuple(
    [(h, p) for h in range(3) for p in order] + [(3, p) for p in order[: NP // 2]]
    for order in (list(range(NP)), list(range(NP))[::-1])
)
NS = len(ORDERS[0])
DEPTH = 4
FIRST = (24, 20)
assert min(FIRST) >= NS - NP // 2 - NP // 2
SIGN = (1, -1)


def source(z, d, steps):
    return lax.rem(z - SIGN[d] * steps + N, N)


def rows_of(p):
    return pl.ds(*PIECES[p])


def late_slot(d, k):
    return 2 if ORDERS[d][k][0] == 3 else d


def exchange(
    wq, lq, hq, wk, lk, hk, wv, lv, hv, nt, ns,
    buf, gain,
    wq_v, wk_v, wv_v, lq_v, lk_v, lv_v, hq_v, hk_v, hv_v, nt_v, ns_v, gains,
    in_sem, send_sem, recv_sem, gsend, grecv, psend, precv, ready,
):
    z = lax.axis_index("rows")
    c = lax.axis_index("cols")
    to = (lax.rem(z + 1, N), lax.rem(z + N - 1, N))
    up, down = lax.rem(c + 2, N), lax.rem(c + N - 2, N)
    odd = lax.rem(c, 2)
    partner = c + 1 - 2 * odd
    barrier = pltpu.get_barrier_semaphore()

    def signal(sem, **who):
        pl.semaphore_signal(sem, inc=1, device_id=who, device_id_type=MESH)

    pl.when(z < N - 1)(lambda: signal(barrier, rows=to[0]))
    pl.when(z == 0)(lambda: signal(barrier, rows=to[1]))
    pl.when(c < N - 2)(lambda: signal(barrier, cols=up))
    pl.when(c < 2)(lambda: signal(barrier, cols=down))
    pl.when(odd == 1)(lambda: signal(barrier, cols=partner))

    count = [0]

    def load(src, dst):
        copy = pltpu.make_async_copy(src, dst, in_sem.at[count[0]])
        copy.start()
        count[0] += 1
        return copy

    got = {6: [load(lv, lv_v), load(hv, hv_v), load(wv, wv_v)]}
    got[0] = [load(lq, lq_v), load(hq, hq_v), load(wq.at[:, pl.ds(0, UNIT)], wq_v.at[0])]
    got[5] = [load(lk, lk_v), load(hk, hk_v), load(wk, wk_v)]
    for i in (1, 4, 2, 3):
        got[i] = [load(wq.at[:, pl.ds(i * UNIT, UNIT)], wq_v.at[i])]
    got_norm = [load(nt, nt_v), load(ns, ns_v)]

    ahead = [z > 0, z == N - 1, c >= 2, c >= N - 2, odd == 0]
    ahead = sum(x.astype(jnp.int32) for x in ahead)
    pl.when(ahead > 0)(lambda: pl.semaphore_wait(barrier, ahead))
    pl.when(z > 0)(lambda: signal(ready.at[0], rows=to[1]))
    pl.when(z == N - 1)(lambda: signal(ready.at[1], rows=to[0]))
    pl.when(c >= 2)(lambda: signal(ready.at[2], cols=down))
    pl.when(odd == 0)(lambda: signal(ready.at[3], cols=partner))

    def greet(d):
        pl.when(z < N - 1 if d == 0 else z == 0)(lambda: pl.semaphore_wait(ready.at[d], 1))

    def compute(i):
        for x in got[i]:
            x.wait()
        w, h, lt = (
            (wq_v[i], hq_v[:, i * UNIT : (i + 1) * UNIT], lq_v[...]) if i < 5
            else (wk_v[...], hk_v[...], lk_v[...]) if i == 5
            else (wv_v[...], hv_v[...], lv_v[...])
        )
        delta = lax.dot_general(h, lt, (((0,), (0,)), ((), ())), preferred_element_type=F32)
        buf[z, pl.ds(i * UNIT, UNIT), :] = (w.T.astype(F32) + MIX * delta).astype(BF16)

    def piece_copy(d, k, steps_more=0):
        hop, p = ORDERS[d][k]
        ref = buf.at[source(z, d, hop + steps_more), rows_of(p), :]
        return pltpu.make_async_remote_copy(
            src_ref=ref, dst_ref=ref, send_sem=send_sem.at[d, k], recv_sem=recv_sem.at[d, k],
            device_id={"rows": to[d]}, device_id_type=MESH,
        )

    def arrived(d, k):
        piece_copy(d, k, 1).wait_recv()

    def gain_copy(d, hop, steps_more=0):
        ref = gains.at[c, source(z, d, hop + steps_more)]
        return pltpu.make_async_remote_copy(
            src_ref=ref, dst_ref=ref, send_sem=gsend.at[d, hop], recv_sem=grecv.at[d, hop],
            device_id={"rows": to[d]}, device_id_type=MESH,
        )

    def partner_copy(col):
        ref = gains.at[col]
        return pltpu.make_async_remote_copy(
            src_ref=ref, dst_ref=ref, send_sem=psend.at[0], recv_sem=precv.at[0],
            device_id={"cols": partner}, device_id_type=MESH,
        )

    def pair_copy(hop, steps_more=0):
        ref = gains.at[pl.ds(lax.rem(c - odd - 2 * (hop + steps_more) + N, N), 2)]
        return pltpu.make_async_remote_copy(
            src_ref=ref, dst_ref=ref, send_sem=psend.at[1 + hop], recv_sem=precv.at[1 + hop],
            device_id={"cols": up}, device_id_type=MESH,
        )

    def norm_step(k):
        if k in (4, 7, 10, 13):
            hop = (k - 4) // 3
            for d in range(2):
                if hop < 4 - d:
                    if hop:
                        gain_copy(d, hop - 1, 1).wait_recv()
                    gain_copy(d, hop).start()
        elif k == 16:
            gain_copy(1, 2, 1).wait_recv()
            gain_copy(0, 3, 1).wait_recv()
            pl.when(odd == 1)(lambda: pl.semaphore_wait(ready.at[3], 1))
            partner_copy(c).start()
        elif k == 17:
            partner_copy(partner).wait_recv()
            pl.when(c < N - 2)(lambda: pl.semaphore_wait(ready.at[2], 1))
            pair_copy(0).start()
        elif k in (18, 19):
            pair_copy(k - 18, 1).wait_recv()
            pair_copy(k - 17).start()

    def norm_end():
        pair_copy(2, 1).wait_recv()
        lane = lax.broadcasted_iota(jnp.int32, (N, PAD), 1)
        rows = [jnp.zeros((N, PAD), F32) for _ in range(5)]
        for j in range(N):
            row, off = divmod(80 * j, PAD)
            v = gains[j].reshape(N, PAD)
            v = pltpu.roll(v, off, 1) if off else v
            rows[row] = jnp.where((lane >= off) & (lane < off + 80), v, rows[row])
            if off + 80 > PAD:
                rows[row + 1] = jnp.where(lane < off + 80 - PAD, v, rows[row + 1])
        for j in range(5):
            gain[pl.ds(j, N, stride=5), :] = rows[j]
        for d in range(2):
            for hop in range(4 - d):
                gain_copy(d, hop).wait_send()
        partner_copy(c).wait_send()
        for hop in range(3):
            pair_copy(hop).wait_send()

    units = (6, 0, 5, 1, 4, 2, 3)

    @pl.when(z == 0)
    def _():
        for i in units:
            compute(i)
        for d in range(2):
            greet(d)
            for k in range(DEPTH):
                piece_copy(d, k).start()

    @pl.when(z > 0)
    def _():
        done = 2
        for i in units[:done]:
            compute(i)
        for k in range(DEPTH):
            for d in (1, 0):
                if k == 0:
                    greet(d)
                piece_copy(d, k).start()
                if done < len(units):
                    compute(units[done])
                    done += 1

    for x in got_norm:
        x.wait()
    gains[c, z, 0:1, 0:80] = (nt_v[...] + ns_v[...]).reshape(1, 80)

    def item(k):
        for d in (1, 0):
            hop, p = ORDERS[d][k]
            if hop:
                arrived(d, k - NP)
            piece_copy(d, k - DEPTH).wait_send()
            piece_copy(d, k).start()

    def drain(last):
        for d in range(2):
            for k in range(last - DEPTH, last):
                piece_copy(d, k).wait_send()
            for k in range(last - NP, last):
                arrived(d, k)

    low, high = sorted(FIRST)
    for k in range(DEPTH, low):
        norm_step(k)
        item(k)
    norm_end()
    for parity in range(2):

        @pl.when(odd == parity)
        def _():
            for k in range(low, FIRST[parity]):
                item(k)
            drain(FIRST[parity])


def finish(buf, late, send_sem, recv_sem):
    z = lax.axis_index("rows")
    odd = lax.rem(lax.axis_index("cols"), 2)
    to = (lax.rem(z + 1, N), lax.rem(z + N - 1, N))
    barrier = pltpu.get_barrier_semaphore()
    for d in range(2):
        pl.semaphore_signal(barrier, inc=1, device_id={"rows": to[d]}, device_id_type=MESH)
    pl.semaphore_wait(barrier, 2)

    def piece_copy(d, k):
        hop, p = ORDERS[d][k]
        return pltpu.make_async_remote_copy(
            src_ref=buf.at[source(z, d, hop), rows_of(p), :], dst_ref=late.at[late_slot(d, k), rows_of(p), :],
            send_sem=send_sem.at[d, k], recv_sem=recv_sem.at[d, k],
            device_id={"rows": to[d]}, device_id_type=MESH,
        )

    def send(k):
        for d in (1, 0):
            piece_copy(d, k).start()

    def wait(k):
        for d in (1, 0):
            piece_copy(d, k).wait()

    low, high = sorted(FIRST)
    pl.when(odd == FIRST.index(low))(lambda: [send(k) for k in range(low, high)] and None)
    for k in range(high, NS):
        send(k)
    pl.when(odd == FIRST.index(low))(lambda: [wait(k) for k in range(low, high)] and None)
    for k in range(high, NS):
        wait(k)


def spans(pieces):
    runs = []
    for p in sorted(pieces):
        first, height = PIECES[p]
        if runs and runs[-1][1] == first and first not in (640, 768):
            runs[-1][1] = first + height
        else:
            runs.append([first, first + height])
    return runs


def write_out(outs, z, sem, jobs):
    copies = []
    for block, distance, pieces in jobs:
        at = pl.ds(pl.multiple_of(lax.rem(z + distance + N, N) * ROWS, ROWS), ROWS)
        for first, last in spans(pieces):
            which = 0 if first < 640 else 1 if first < 768 else 2
            copies.append(
                pltpu.make_async_copy(
                    block.at[pl.ds(first, last - first), :],
                    outs[which].at[pl.ds(first - sum(COLS[:which]), last - first), at],
                    sem.at[len(copies)],
                )
            )
    for copy in copies:
        copy.start()
    for copy in copies:
        copy.wait()


def arrivals(ks):
    blocks = {}
    for d in range(2):
        for k in ks:
            hop, p = ORDERS[d][k]
            distance = -SIGN[d] * (hop + 1)
            blocks.setdefault(4 if distance == -4 else distance, []).append(p)
    return blocks


def deliver(buf, gain, q, k, v, g, sem):
    z = lax.axis_index("rows")
    odd = lax.rem(lax.axis_index("cols"), 2)
    g[...] = gain[...].astype(BF16)
    for parity in range(2):

        @pl.when(odd == parity)
        def _():
            blocks = {0: list(range(NP))} | arrivals(range(FIRST[parity]))
            write_out((q, k, v), z, sem, [(buf.at[lax.rem(z + b + N, N)], b, ps) for b, ps in blocks.items()])


def deliver_late(late, q_in, k_in, v_in, q, k, v, sem):
    z = lax.axis_index("rows")
    odd = lax.rem(lax.axis_index("cols"), 2)
    slots = {-3: 0, 3: 1, 4: 2}
    for parity in range(2):

        @pl.when(odd == parity)
        def _():
            blocks = arrivals(range(FIRST[parity], NS))
            write_out((q, k, v), z, sem, [(late.at[slots[b]], b, ps) for b, ps in blocks.items()])


def local(wq, lq, hq, wk, lk, hk, wv, lv, hv, nt, ns):
    hbm = pl.BlockSpec(memory_space=pltpu.HBM)
    vmem = pl.BlockSpec(memory_space=pltpu.VMEM)
    dma = pltpu.SemaphoreType.DMA
    limit = 16 << 20
    args = (wq, lq.T, hq, wk, lk.T, hk, wv, lv.T, hv, nt, ns)
    buf, gain = pl.pallas_call(
        exchange,
        name="exchange",
        out_shape=(
            jax.ShapeDtypeStruct((N, WIDTH, ROWS), BF16),
            jax.ShapeDtypeStruct((40, PAD), F32),
        ),
        in_specs=[hbm] * 11,
        out_specs=(vmem, vmem),
        scratch_shapes=[
            pltpu.VMEM((5, ROWS, UNIT), BF16),
            pltpu.VMEM((ROWS, UNIT), BF16),
            pltpu.VMEM((ROWS, UNIT), BF16),
            pltpu.VMEM((32, ROWS), BF16),
            pltpu.VMEM((32, ROWS), BF16),
            pltpu.VMEM((32, ROWS), BF16),
            pltpu.VMEM((32, COLS[0]), BF16),
            pltpu.VMEM((32, COLS[1]), BF16),
            pltpu.VMEM((32, COLS[2]), BF16),
            pltpu.VMEM((80,), F32),
            pltpu.VMEM((80,), F32),
            pltpu.VMEM((N, N, 1, PAD), F32),
            dma((16,)),
            dma((2, NS)),
            dma((2, NS)),
            dma((2, 4)),
            dma((2, 4)),
            dma((4,)),
            dma((4,)),
            pltpu.SemaphoreType.REGULAR((4,)),
        ],
        compiler_params=pltpu.CompilerParams(collective_id=0, has_side_effects=True, vmem_limit_bytes=limit),
    )(*(pltpu.with_memory_space_constraint(x, pltpu.HBM) for x in args))
    wide = [jax.ShapeDtypeStruct((width, N * ROWS), BF16) for width in COLS]
    q, k, v, g = pl.pallas_call(
        deliver,
        name="deliver",
        out_shape=(*wide, jax.ShapeDtypeStruct((40, PAD), BF16)),
        in_specs=[vmem, vmem],
        out_specs=(hbm, hbm, hbm, vmem),
        scratch_shapes=[dma((32,))],
        compiler_params=pltpu.CompilerParams(vmem_limit_bytes=limit, has_side_effects=True),
    )(buf, gain)
    late = pl.pallas_call(
        finish,
        name="finish",
        out_shape=jax.ShapeDtypeStruct((3, WIDTH, ROWS), BF16),
        in_specs=[vmem],
        out_specs=vmem,
        scratch_shapes=[dma((2, NS)), dma((2, NS))],
        compiler_params=pltpu.CompilerParams(collective_id=1, has_side_effects=True, vmem_limit_bytes=limit),
    )(buf)
    q, k, v = pl.pallas_call(
        deliver_late,
        name="deliver_late",
        out_shape=tuple(wide),
        in_specs=[vmem, hbm, hbm, hbm],
        out_specs=(hbm, hbm, hbm),
        scratch_shapes=[dma((16,))],
        input_output_aliases={1: 0, 2: 1, 3: 2},
        compiler_params=pltpu.CompilerParams(vmem_limit_bytes=limit),
    )(late, q, k, v)
    return q, k, v, g.reshape(N * ROWS)


def solution(mesh):
    return jax.shard_map(
        local,
        mesh=mesh,
        in_specs=(
            P(("trial", "rows"), "cols"),
            P(("trial", "rows"), None),
            P("trial", "cols"),
            P(("trial", "rows"), "cols"),
            P(("trial", "rows"), None),
            P("trial", "cols"),
            P(("trial", "rows"), "cols"),
            P(("trial", "rows"), None),
            P("trial", "cols"),
            P(("trial", "rows", "cols")),
            P(("trial", "rows", "cols")),
        ),
        out_specs=(
            P(("trial", "cols"), None),
            P(("trial", "cols"), None),
            P(("trial", "cols"), None),
            P("trial"),
        ),
        check_vma=False,
    )
```

time: 134 us -> 99.6 us (0.74); the launches traced: 132 us -> 99.5 us
  Pallas kernels: 0 us -> 98.8 us
  waiting for transfers between devices: 84 us -> 0 us
  blocking collectives: 19.6 us -> 0 us
  between operations: 14.2 us -> 0.66 us
  local copies, waits for them, and re-layouts: 12.4 us -> 0 us
    pallas_call x0 -> x4, Pallas kernels: none -> 98.8 us  [the longest x1 77.5 us: local(): pl.pallas_call(exchange, name='exchange', out_shape=(jax.ShapeDtypeStruct...]
    all_gather x1 -> x0, waiting for transfers between devices: 84 us -> none  [in_one_piece(): result = lax.all_gather(both, axis, axis=dim, tiled=True)]
    all_to_all x1 -> x0, blocking collectives: 19.6 us -> none  [from_everyone(): return lax.all_to_all(copies, axis, split_axis=0, concat_axis=0, tiled=True)]
    transpose x2 -> x0, local copies, waits for them, and re-layouts: 9.44 us -> none  [local(): serve_query, serve_key, serve_value = (serve_query.T, serve_key.T, serve_...]
    unnamed x23 -> x0, local copies, waits for them, and re-layouts: 2.28 us -> none
  transfers between devices with their start and end apart: 1 -> 0, of which waited for: 1 -> 0; matrix products, arithmetic and copies ran while one was open for 1% -> 0% of each run, Pallas kernels for 0% -> 0%
where the time goes in v2:
time: 99.6 us; the launch traced here: 99.5 us
  Pallas kernels  98.8 us (99%)
    pallas_call x1, Pallas kernels, local(): pl.pallas_call(exchange, name='exchange', out_shape=(jax.ShapeDtypeStruct...  77.5 us
    pallas_call x1, Pallas kernels, local(): pl.pallas_call(finish, name='finish', out_shape=jax.ShapeDtypeStruct((3,...  16.1 us
    pallas_call x1, Pallas kernels, local(): pl.pallas_call(deliver, name='deliver', out_shape=(*wide, jax.ShapeDtypeS...  4.05 us

profile of v2, /device:TPU:24, one launch (start us, length us, event | category | flops | bytes accessed | tf_op | source)
XLA Modules:
  0.0 99.5 jit_solution(4790602417215398627)
XLA Ops:
  0.6 77.5 %exchange.1 = (bf16[8,896,640]{2,1,0:T(8,128)(2,1)S(1)}, f32[40,128]{1,0:T(8,128)S(1)}) custom-call(bf16[640,640]{1,0:T(8,128)(2,1)} %wq.1, bf16[32,640]{1,0:T(8,128)(2,1)} %bitcast.4, bf16[32,640]{1,0:T(8,128)(2,1)} %hq.1, bf16[640,128]{1,0:T(8,128)(2,1)} %wk.1, bf16[32,640]{1,0:T(8,128)(2,1)} %bitcast.5, bf16[32,128]{1,0:T(8,128)(2,1)} %hk.1, ...), custom_call_target="tpu_custom_call" | custom-call | tf_op jit(solution)/shard_map/exchange/pallas_call | solution.py:342
  78.1 4.0 %deliver.1 = (bf16[640,5120]{1,0:T(8,128)(2,1)}, bf16[128,5120]{1,0:T(8,128)(2,1)}, bf16[128,5120]{1,0:T(8,128)(2,1)}, bf16[40,128]{1,0:T(8,128)(2,1)}) custom-call(bf16[8,896,640]{2,1,0:T(8,128)(2,1)S(1)} %get-tuple-element.13.buf, f32[40,128]{1,0:T(8,128)S(1)} %get-tuple-element.14.gain), custom_call_target="tpu_custom_call" | custom-call | tf_op jit(solution)/shard_map/deliver/pallas_call | solution.py:376
  82.2 16.1 %finish.1.late = bf16[3,896,640]{2,1,0:T(8,128)(2,1)S(1)} custom-call(bf16[8,896,640]{2,1,0:T(8,128)(2,1)S(1)} %get-tuple-element.13.buf), custom_call_target="tpu_custom_call" | custom-call | tf_op jit(solution)/shard_map/finish/pallas_call | solution.py:385
  98.3 1.1 %deliver_late.1 = (bf16[640,5120]{1,0:T(8,128)(2,1)}, bf16[128,5120]{1,0:T(8,128)(2,1)}, bf16[128,5120]{1,0:T(8,128)(2,1)}) custom-call(bf16[3,896,640]{2,1,0:T(8,128)(2,1)S(1)} %finish.1.late, bf16[640,5120]{1,0:T(8,128)(2,1)} %get-tuple-element.15.q_in, ...), custom_call_target="tpu_custom_call", output_to_operand_aliasing={{0}: (1, {}), {1}: (2, {}), {2}: (3, {})} | custom-call | tf_op jit(solution)/shard_map/deliver_late/pallas_call | solution.py:394

commit v3 on v2

--- a/solution.py
+++ b/solution.py
@@ -18,17 +18,19 @@
 WIDTH = sum(COLS)
 PAD = 128
 UNIT = 128
-PIECES = ((0, 128), (128, 128), (256, 128), (384, 64), (448, 64), (512, 128), (640, 128), (768, 128))
-NP = len(PIECES)
-UNIT_OF = (0, 1, 2, 3, 3, 4, 5, 6)
-ORDERS = tuple(
-    [(h, p) for h in range(3) for p in order] + [(3, p) for p in order[: NP // 2]]
-    for order in (list(range(NP)), list(range(NP))[::-1])
+HOPS = (
+    ((0, 128), (128, 320), (448, 320), (768, 128)),
+    ((0, 128), (128, 320), (448, 448)),
+    ((0, 448), (448, 448)),
+    ((0, 384), (384, 64)),
 )
-NS = len(ORDERS[0])
-DEPTH = 4
-FIRST = (24, 20)
-assert min(FIRST) >= NS - NP // 2 - NP // 2
+RIGHT = [(h, *piece) for h, pieces in enumerate(HOPS) for piece in pieces]
+LEFT = [(h, WIDTH - first - height, height) for h, first, height in RIGHT[:-2]] + [(3, 448, 448), (3, 384, 64)]
+ORDERS = (RIGHT, LEFT)
+NS = len(RIGHT)
+LAST = NS - 1
+DEPTH = 2
+FIRST = (9, 7)
 SIGN = (1, -1)
 
 
@@ -36,12 +38,30 @@
     return lax.rem(z - SIGN[d] * steps + N, N)
 
 
-def rows_of(p):
-    return pl.ds(*PIECES[p])
-
-
-def late_slot(d, k):
-    return 2 if ORDERS[d][k][0] == 3 else d
+def rows_of(d, k):
+    return pl.ds(*ORDERS[d][k][1:])
+
+
+def needs(d, k):
+    hop, first, height = ORDERS[d][k]
+    return [
+        i for i, (h, f, n) in enumerate(ORDERS[d])
+        if h == hop - 1 and f < first + height and first < f + n
+    ]
+
+
+def if_sent(z, d, k, act):
+    if k < LAST:
+        act()
+    else:
+        pl.when(z < N - 1 if d == 0 else z == 1)(act)
+
+
+def if_received(z, d, k, act):
+    if k < LAST:
+        act()
+    else:
+        pl.when(z > 0 if d == 0 else z == 0)(act)
 
 
 def exchange(
@@ -105,15 +125,11 @@
         buf[z, pl.ds(i * UNIT, UNIT), :] = (w.T.astype(F32) + MIX * delta).astype(BF16)
 
     def piece_copy(d, k, steps_more=0):
-        hop, p = ORDERS[d][k]
-        ref = buf.at[source(z, d, hop + steps_more), rows_of(p), :]
+        ref = buf.at[source(z, d, ORDERS[d][k][0] + steps_more), rows_of(d, k), :]
         return pltpu.make_async_remote_copy(
             src_ref=ref, dst_ref=ref, send_sem=send_sem.at[d, k], recv_sem=recv_sem.at[d, k],
             device_id={"rows": to[d]}, device_id_type=MESH,
         )
-
-    def arrived(d, k):
-        piece_copy(d, k, 1).wait_recv()
 
     def gain_copy(d, hop, steps_more=0):
         ref = gains.at[c, source(z, d, hop + steps_more)]
@@ -137,28 +153,22 @@
         )
 
     def norm_step(k):
-        if k in (4, 7, 10, 13):
-            hop = (k - 4) // 3
-            for d in range(2):
-                if hop < 4 - d:
-                    if hop:
-                        gain_copy(d, hop - 1, 1).wait_recv()
-                    gain_copy(d, hop).start()
-        elif k == 16:
-            gain_copy(1, 2, 1).wait_recv()
-            gain_copy(0, 3, 1).wait_recv()
-            pl.when(odd == 1)(lambda: pl.semaphore_wait(ready.at[3], 1))
-            partner_copy(c).start()
-        elif k == 17:
-            partner_copy(partner).wait_recv()
-            pl.when(c < N - 2)(lambda: pl.semaphore_wait(ready.at[2], 1))
-            pair_copy(0).start()
-        elif k in (18, 19):
-            pair_copy(k - 18, 1).wait_recv()
-            pair_copy(k - 17).start()
+        hop = {2: 1, 3: 2, 5: 3}.get(k)
+        for d in range(2):
+            if hop is not None and hop < 4 - d:
+                gain_copy(d, hop - 1, 1).wait_recv()
+                gain_copy(d, hop).start()
 
     def norm_end():
-        pair_copy(2, 1).wait_recv()
+        gain_copy(1, 2, 1).wait_recv()
+        gain_copy(0, 3, 1).wait_recv()
+        pl.when(odd == 1)(lambda: pl.semaphore_wait(ready.at[3], 1))
+        partner_copy(c).start()
+        partner_copy(partner).wait_recv()
+        pl.when(c < N - 2)(lambda: pl.semaphore_wait(ready.at[2], 1))
+        for hop in range(3):
+            pair_copy(hop).start()
+            pair_copy(hop, 1).wait_recv()
         lane = lax.broadcasted_iota(jnp.int32, (N, PAD), 1)
         rows = [jnp.zeros((N, PAD), F32) for _ in range(5)]
         for j in range(N):
@@ -177,62 +187,66 @@
         for hop in range(3):
             pair_copy(hop).wait_send()
 
-    units = (6, 0, 5, 1, 4, 2, 3)
-
-    @pl.when(z == 0)
-    def _():
-        for i in units:
-            compute(i)
-        for d in range(2):
-            greet(d)
-            for k in range(DEPTH):
-                piece_copy(d, k).start()
-
-    @pl.when(z > 0)
-    def _():
-        done = 2
-        for i in units[:done]:
-            compute(i)
-        for k in range(DEPTH):
-            for d in (1, 0):
-                if k == 0:
-                    greet(d)
-                piece_copy(d, k).start()
-                if done < len(units):
-                    compute(units[done])
-                    done += 1
+    def begin(d):
+        greet(d)
+        gain_copy(d, 0).start()
+        piece_copy(d, 0).start()
 
     for x in got_norm:
         x.wait()
     gains[c, z, 0:1, 0:80] = (nt_v[...] + ns_v[...]).reshape(1, 80)
 
-    def item(k):
+    @pl.when(z == 0)
+    def _():
+        for i in (0, 6, 1, 2, 3, 4, 5):
+            compute(i)
+        for d in range(2):
+            begin(d)
+            piece_copy(d, 1).start()
+
+    @pl.when(z > 0)
+    def _():
+        for i in (6, 0, 5):
+            compute(i)
+        begin(1)
+        compute(1)
+        begin(0)
+        for i in (4, 2, 3):
+            compute(i)
         for d in (1, 0):
-            hop, p = ORDERS[d][k]
-            if hop:
-                arrived(d, k - NP)
+            piece_copy(d, 1).start()
+
+    def item(k, met):
+        for d in (1, 0):
+            for i in needs(d, k):
+                if (d, i) not in met:
+                    piece_copy(d, i, 1).wait_recv()
+                    met.add((d, i))
             piece_copy(d, k - DEPTH).wait_send()
             piece_copy(d, k).start()
 
-    def drain(last):
+    def drain(last, met):
         for d in range(2):
             for k in range(last - DEPTH, last):
                 piece_copy(d, k).wait_send()
-            for k in range(last - NP, last):
-                arrived(d, k)
-
-    low, high = sorted(FIRST)
+            for k in range(last):
+                if (d, k) not in met:
+                    piece_copy(d, k, 1).wait_recv()
+
+    met = set()
+    low = min(FIRST)
     for k in range(DEPTH, low):
         norm_step(k)
-        item(k)
+        item(k, met)
     norm_end()
     for parity in range(2):
 
         @pl.when(odd == parity)
         def _():
+            mine = set(met)
             for k in range(low, FIRST[parity]):
-                item(k)
-            drain(FIRST[parity])
+                item(k, mine)
+            drain(FIRST[parity], mine)
 
 
 def finish(buf, late, send_sem, recv_sem):
@@ -244,69 +258,50 @@
         pl.semaphore_signal(barrier, inc=1, device_id={"rows": to[d]}, device_id_type=MESH)
     pl.semaphore_wait(barrier, 2)
 
-    def piece_copy(d, k):
-        hop, p = ORDERS[d][k]
+    def piece_copy(d, k, first):
+        hop = ORDERS[d][k][0]
+        here = late.at[d] if needs(d, k)[0] >= first else buf.at[source(z, d, hop)]
         return pltpu.make_async_remote_copy(
-            src_ref=buf.at[source(z, d, hop), rows_of(p), :], dst_ref=late.at[late_slot(d, k), rows_of(p), :],
+            src_ref=here.at[rows_of(d, k), :], dst_ref=late.at[2 if hop == 3 else d, rows_of(d, k), :],
             send_sem=send_sem.at[d, k], recv_sem=recv_sem.at[d, k],
             device_id={"rows": to[d]}, device_id_type=MESH,
         )
 
-    def send(k):
-        for d in (1, 0):
-            piece_copy(d, k).start()
-
-    def wait(k):
-        for d in (1, 0):
-            piece_copy(d, k).wait()
-
-    low, high = sorted(FIRST)
-    pl.when(odd == FIRST.index(low))(lambda: [send(k) for k in range(low, high)] and None)
-    for k in range(high, NS):
-        send(k)
-    pl.when(odd == FIRST.index(low))(lambda: [wait(k) for k in range(low, high)] and None)
-    for k in range(high, NS):
-        wait(k)
-
-
-def spans(pieces):
-    runs = []
-    for p in sorted(pieces):
-        first, height = PIECES[p]
-        if runs and runs[-1][1] == first and first not in (640, 768):
-            runs[-1][1] = first + height
-        else:
-            runs.append([first, first + height])
-    return runs
-
-
-def write_out(outs, z, sem, jobs):
+    for parity, first in enumerate(FIRST):
+
+        @pl.when(odd == parity)
+        def _():
+            met = set()
+            for k in range(first, NS):
+                for d in (1, 0):
+                    for i in needs(d, k):
+                        if i >= first and (d, i) not in met:
+                            piece_copy(d, i, first).wait_recv()
+                            met.add((d, i))
+                    if_sent(z, d, k, lambda d=d, k=k: piece_copy(d, k, first).start())
+            for k in range(first, NS):
+                for d in (1, 0):
+                    if_sent(z, d, k, lambda d=d, k=k: piece_copy(d, k, first).wait_send())
+                    if (d, k) not in met:
+                        if_received(z, d, k, lambda d=d, k=k: piece_copy(d, k, first).wait_recv())
+
+
+def write_out(outs, z, sem, blocks):
     copies = []
-    for block, distance, pieces in jobs:
+    for block, distance in blocks:
         at = pl.ds(pl.multiple_of(lax.rem(z + distance + N, N) * ROWS, ROWS), ROWS)
-        for first, last in spans(pieces):
-            which = 0 if first < 640 else 1 if first < 768 else 2
-            copies.append(
-                pltpu.make_async_copy(
-                    block.at[pl.ds(first, last - first), :],
-                    outs[which].at[pl.ds(first - sum(COLS[:which]), last - first), at],
-                    sem.at[len(copies)],
-                )
-            )
+        first = 0
+        for out, width in zip(outs, COLS):
+            copies.append(pltpu.make_async_copy(block.at[pl.ds(first, width), :], out.at[:, at], sem.at[len(copies)]))
+            first += width
     for copy in copies:
         copy.start()
     for copy in copies:
         copy.wait()
 
 
-def arrivals(ks):
-    blocks = {}
-    for d in range(2):
-        for k in ks:
-            hop, p = ORDERS[d][k]
-            distance = -SIGN[d] * (hop + 1)
-            blocks.setdefault(4 if distance == -4 else distance, []).append(p)
-    return blocks
+def early(parity):
+    return (0, 1, -1, 2, -2) if FIRST[parity] == 7 else (0, 1, -1, 2, -2, 3, -3)
 
 
 def deliver(buf, gain, q, k, v, g, sem):
@@ -317,20 +312,18 @@
 
         @pl.when(odd == parity)
         def _():
-            blocks = {0: list(range(NP))} | arrivals(range(FIRST[parity]))
-            write_out((q, k, v), z, sem, [(buf.at[lax.rem(z + b + N, N)], b, ps) for b, ps in blocks.items()])
+            write_out((q, k, v), z, sem, [(buf.at[lax.rem(z + b + N, N)], b) for b in early(parity)])
 
 
 def deliver_late(late, q_in, k_in, v_in, q, k, v, sem):
     z = lax.axis_index("rows")
     odd = lax.rem(lax.axis_index("cols"), 2)
-    slots = {-3: 0, 3: 1, 4: 2}
     for parity in range(2):
 
         @pl.when(odd == parity)
         def _():
-            blocks = arrivals(range(FIRST[parity], NS))
-            write_out((q, k, v), z, sem, [(late.at[slots[b]], b, ps) for b, ps in blocks.items()])
+            blocks = [(late.at[slot], b) for slot, b in enumerate((-3, 3, 4)) if b not in early(parity)]
+            write_out((q, k, v), z, sem, blocks)
 
 
 def local(wq, lq, hq, wk, lk, hk, wv, lv, hv, nt, ns):

time: 99.6 us -> 95.6 us (0.960)
  Pallas kernels: 98.8 us -> 94.8 us
    pallas_call x1, Pallas kernels: 16.1 us -> 13.5 us  [local(): pl.pallas_call(finish, name='finish', out_shape=jax.ShapeDtypeStruct((3,...]
    pallas_call x1, Pallas kernels: 77.5 us -> 76.1 us  [local(): pl.pallas_call(exchange, name='exchange', out_shape=(jax.ShapeDtypeStruct...]
where the time goes in v3:
time: 95.6 us; the launch traced here: 95.4 us
  Pallas kernels  94.8 us (99%)
    pallas_call x1, Pallas kernels, local(): pl.pallas_call(exchange, name='exchange', out_shape=(jax.ShapeDtypeStruct...  76.1 us
    pallas_call x1, Pallas kernels, local(): pl.pallas_call(finish, name='finish', out_shape=jax.ShapeDtypeStruct((3,...  13.5 us
    pallas_call x1, Pallas kernels, local(): pl.pallas_call(deliver, name='deliver', out_shape=(*wide, jax.ShapeDtypeS...  4.05 us

profile of v3, /device:TPU:24, one launch (start us, length us, event | category | flops | bytes accessed | tf_op | source)
XLA Modules:
  0.0 95.4 jit_solution(8826178982075056638)
XLA Ops:
  0.6 76.1 %exchange.1 = (bf16[8,896,640]{2,1,0:T(8,128)(2,1)S(1)}, f32[40,128]{1,0:T(8,128)S(1)}) custom-call(bf16[640,640]{1,0:T(8,128)(2,1)} %wq.1, bf16[32,640]{1,0:T(8,128)(2,1)} %bitcast.4, bf16[32,640]{1,0:T(8,128)(2,1)} %hq.1, bf16[640,128]{1,0:T(8,128)(2,1)} %wk.1, bf16[32,640]{1,0:T(8,128)(2,1)} %bitcast.5, bf16[32,128]{1,0:T(8,128)(2,1)} %hk.1, ...), custom_call_target="tpu_custom_call" | custom-call | tf_op jit(solution)/shard_map/exchange/pallas_call | solution.py:335
  76.7 4.0 %deliver.1 = (bf16[640,5120]{1,0:T(8,128)(2,1)}, bf16[128,5120]{1,0:T(8,128)(2,1)}, bf16[128,5120]{1,0:T(8,128)(2,1)}, bf16[40,128]{1,0:T(8,128)(2,1)}) custom-call(bf16[8,896,640]{2,1,0:T(8,128)(2,1)S(1)} %get-tuple-element.13.buf, f32[40,128]{1,0:T(8,128)S(1)} %get-tuple-element.14.gain), custom_call_target="tpu_custom_call" | custom-call | tf_op jit(solution)/shard_map/deliver/pallas_call | solution.py:369
  80.8 13.5 %finish.1.late = bf16[3,896,640]{2,1,0:T(8,128)(2,1)S(1)} custom-call(bf16[8,896,640]{2,1,0:T(8,128)(2,1)S(1)} %get-tuple-element.13.buf), custom_call_target="tpu_custom_call" | custom-call | tf_op jit(solution)/shard_map/finish/pallas_call | solution.py:378
  94.3 1.1 %deliver_late.1 = (bf16[640,5120]{1,0:T(8,128)(2,1)}, bf16[128,5120]{1,0:T(8,128)(2,1)}, bf16[128,5120]{1,0:T(8,128)(2,1)}) custom-call(bf16[3,896,640]{2,1,0:T(8,128)(2,1)S(1)} %finish.1.late, bf16[640,5120]{1,0:T(8,128)(2,1)} %get-tuple-element.15.q_in, ...), custom_call_target="tpu_custom_call", output_to_operand_aliasing={{0}: (1, {}), {1}: (2, {}), {2}: (3, {})} | custom-call | tf_op jit(solution)/shard_map/deliver_late/pallas_call | solution.py:387

commit v4 on v3

--- a/solution.py
+++ b/solution.py
@@ -22,10 +22,10 @@
     ((0, 128), (128, 320), (448, 320), (768, 128)),
     ((0, 128), (128, 320), (448, 448)),
     ((0, 448), (448, 448)),
-    ((0, 384), (384, 64)),
+    ((0, 368), (368, 80)),
 )
 RIGHT = [(h, *piece) for h, pieces in enumerate(HOPS) for piece in pieces]
-LEFT = [(h, WIDTH - first - height, height) for h, first, height in RIGHT[:-2]] + [(3, 448, 448), (3, 384, 64)]
+LEFT = [(h, WIDTH - first - height, height) for h, first, height in RIGHT[:-2]] + [(3, 448, 448), (3, 368, 80)]
 ORDERS = (RIGHT, LEFT)
 NS = len(RIGHT)
 LAST = NS - 1
@@ -97,10 +97,36 @@
 
     got = {6: [load(lv, lv_v), load(hv, hv_v), load(wv, wv_v)]}
     got[0] = [load(lq, lq_v), load(hq, hq_v), load(wq.at[:, pl.ds(0, UNIT)], wq_v.at[0])]
+    got_norm = [load(nt, nt_v), load(ns, ns_v)]
     got[5] = [load(lk, lk_v), load(hk, hk_v), load(wk, wk_v)]
     for i in (1, 4, 2, 3):
         got[i] = [load(wq.at[:, pl.ds(i * UNIT, UNIT)], wq_v.at[i])]
-    got_norm = [load(nt, nt_v), load(ns, ns_v)]
+
+    def greet(d):
+        pl.when(z < N - 1 if d == 0 else z == 0)(lambda: pl.semaphore_wait(ready.at[d], 1))
+
+    def compute(i):
+        for x in got[i]:
+            x.wait()
+        w, h, lt = (
+            (wq_v[i], hq_v[:, i * UNIT : (i + 1) * UNIT], lq_v[...]) if i < 5
+            else (wk_v[...], hk_v[...], lk_v[...]) if i == 5
+            else (wv_v[...], hv_v[...], lv_v[...])
+        )
+        delta = lax.dot_general(h, lt, (((0,), (0,)), ((), ())), preferred_element_type=F32)
+        buf[z, pl.ds(i * UNIT, UNIT), :] = (w.T.astype(F32) + MIX * delta).astype(BF16)
+
+    rightmost = (z == 0) | (z == N - 1)
+
+    @pl.when(rightmost)
+    def _():
+        compute(0)
+        compute(6)
+
+    @pl.when(jnp.logical_not(rightmost))
+    def _():
+        compute(6)
+        compute(0)
 
     ahead = [z > 0, z == N - 1, c >= 2, c >= N - 2, odd == 0]
     ahead = sum(x.astype(jnp.int32) for x in ahead)
@@ -109,20 +135,6 @@
     pl.when(z == N - 1)(lambda: signal(ready.at[1], rows=to[0]))
     pl.when(c >= 2)(lambda: signal(ready.at[2], cols=down))
     pl.when(odd == 0)(lambda: signal(ready.at[3], cols=partner))
-
-    def greet(d):
-        pl.when(z < N - 1 if d == 0 else z == 0)(lambda: pl.semaphore_wait(ready.at[d], 1))
-
-    def compute(i):
-        for x in got[i]:
-            x.wait()
-        w, h, lt = (
-            (wq_v[i], hq_v[:, i * UNIT : (i + 1) * UNIT], lq_v[...]) if i < 5
-            else (wk_v[...], hk_v[...], lk_v[...]) if i == 5
-            else (wv_v[...], hv_v[...], lv_v[...])
-        )
-        delta = lax.dot_general(h, lt, (((0,), (0,)), ((), ())), preferred_element_type=F32)
-        buf[z, pl.ds(i * UNIT, UNIT), :] = (w.T.astype(F32) + MIX * delta).astype(BF16)
 
     def piece_copy(d, k, steps_more=0):
         ref = buf.at[source(z, d, ORDERS[d][k][0] + steps_more), rows_of(d, k), :]
@@ -189,32 +201,48 @@
 
     def begin(d):
         greet(d)
+        piece_copy(d, 0).start()
+
+    def more(d):
         gain_copy(d, 0).start()
-        piece_copy(d, 0).start()
-
-    for x in got_norm:
-        x.wait()
-    gains[c, z, 0:1, 0:80] = (nt_v[...] + ns_v[...]).reshape(1, 80)
+        piece_copy(d, 1).start()
+
+    def share_norm():
+        for x in got_norm:
+            x.wait()
+        gains[c, z, 0:1, 0:80] = (nt_v[...] + ns_v[...]).reshape(1, 80)
 
     @pl.when(z == 0)
     def _():
-        for i in (0, 6, 1, 2, 3, 4, 5):
+        begin(0)
+        share_norm()
+        for i in (5, 1, 4, 2, 3):
             compute(i)
-        for d in range(2):
-            begin(d)
-            piece_copy(d, 1).start()
-
-    @pl.when(z > 0)
+        more(0)
+        begin(1)
+        more(1)
+
+    @pl.when(z == N - 1)
     def _():
-        for i in (6, 0, 5):
+        begin(0)
+        compute(5)
+        begin(1)
+        share_norm()
+        for i in (1, 4, 2, 3):
             compute(i)
+        more(0)
+        more(1)
+
+    @pl.when(jnp.logical_not(rightmost))
+    def _():
         begin(1)
-        compute(1)
+        compute(5)
         begin(0)
-        for i in (4, 2, 3):
+        share_norm()
+        for i in (1, 4, 2, 3):
             compute(i)
-        for d in (1, 0):
-            piece_copy(d, 1).start()
+        more(1)
+        more(0)
 
     def item(k, met):
         for d in (1, 0):

time: 95.6 us -> 95.9 us (level)
    pallas_call x1, Pallas kernels: 13.5 us -> 14.5 us  [local(): pl.pallas_call(finish, name='finish', out_shape=jax.ShapeDtypeStruct((3,...]
where the time goes in v4:
time: 95.9 us; the launch traced here: 95.8 us
  Pallas kernels  95.2 us (99%)
    pallas_call x1, Pallas kernels, local(): pl.pallas_call(exchange, name='exchange', out_shape=(jax.ShapeDtypeStruct...  75.5 us
    pallas_call x1, Pallas kernels, local(): pl.pallas_call(finish, name='finish', out_shape=jax.ShapeDtypeStruct((3,...  14.5 us
    pallas_call x1, Pallas kernels, local(): pl.pallas_call(deliver, name='deliver', out_shape=(*wide, jax.ShapeDtypeS...  4.05 us

profile of v4, /device:TPU:24, one launch (start us, length us, event | category | flops | bytes accessed | tf_op | source)
XLA Modules:
  0.0 95.8 jit_solution(14594831653879802200)
XLA Ops:
  0.6 75.5 %exchange.1 = (bf16[8,896,640]{2,1,0:T(8,128)(2,1)S(1)}, f32[40,128]{1,0:T(8,128)S(1)}) custom-call(bf16[640,640]{1,0:T(8,128)(2,1)} %wq.1, bf16[32,640]{1,0:T(8,128)(2,1)} %bitcast.4, bf16[32,640]{1,0:T(8,128)(2,1)} %hq.1, bf16[640,128]{1,0:T(8,128)(2,1)} %wk.1, bf16[32,640]{1,0:T(8,128)(2,1)} %bitcast.5, bf16[32,128]{1,0:T(8,128)(2,1)} %hk.1, ...), custom_call_target="tpu_custom_call" | custom-call | tf_op jit(solution)/shard_map/exchange/pallas_call | solution.py:363
  76.2 4.0 %deliver.1 = (bf16[640,5120]{1,0:T(8,128)(2,1)}, bf16[128,5120]{1,0:T(8,128)(2,1)}, bf16[128,5120]{1,0:T(8,128)(2,1)}, bf16[40,128]{1,0:T(8,128)(2,1)}) custom-call(bf16[8,896,640]{2,1,0:T(8,128)(2,1)S(1)} %get-tuple-element.13.buf, f32[40,128]{1,0:T(8,128)S(1)} %get-tuple-element.14.gain), custom_call_target="tpu_custom_call" | custom-call | tf_op jit(solution)/shard_map/deliver/pallas_call | solution.py:397
  80.2 14.5 %finish.1.late = bf16[3,896,640]{2,1,0:T(8,128)(2,1)S(1)} custom-call(bf16[8,896,640]{2,1,0:T(8,128)(2,1)S(1)} %get-tuple-element.13.buf), custom_call_target="tpu_custom_call" | custom-call | tf_op jit(solution)/shard_map/finish/pallas_call | solution.py:406
  94.7 1.1 %deliver_late.1 = (bf16[640,5120]{1,0:T(8,128)(2,1)}, bf16[128,5120]{1,0:T(8,128)(2,1)}, bf16[128,5120]{1,0:T(8,128)(2,1)}) custom-call(bf16[3,896,640]{2,1,0:T(8,128)(2,1)S(1)} %finish.1.late, bf16[640,5120]{1,0:T(8,128)(2,1)} %get-tuple-element.15.q_in, ...), custom_call_target="tpu_custom_call", output_to_operand_aliasing={{0}: (1, {}), {1}: (2, {}), {2}: (3, {})} | custom-call | tf_op jit(solution)/shard_map/deliver_late/pallas_call | solution.py:415

commit v5 on v4

--- a/solution.py
+++ b/solution.py
@@ -19,18 +19,18 @@
 PAD = 128
 UNIT = 128
 HOPS = (
-    ((0, 128), (128, 320), (448, 320), (768, 128)),
     ((0, 128), (128, 320), (448, 448)),
     ((0, 448), (448, 448)),
-    ((0, 368), (368, 80)),
+    ((0, 448), (448, 448)),
+    ((0, 384), (384, 64)),
 )
 RIGHT = [(h, *piece) for h, pieces in enumerate(HOPS) for piece in pieces]
-LEFT = [(h, WIDTH - first - height, height) for h, first, height in RIGHT[:-2]] + [(3, 448, 448), (3, 368, 80)]
+LEFT = [(h, WIDTH - first - height, height) for h, first, height in RIGHT[:-2]] + [(3, 448, 448), (3, 384, 64)]
 ORDERS = (RIGHT, LEFT)
 NS = len(RIGHT)
 LAST = NS - 1
 DEPTH = 2
-FIRST = (9, 7)
+FIRST = (7, 5)
 SIGN = (1, -1)
 
 
@@ -128,6 +128,10 @@
         compute(6)
         compute(0)
 
+    for x in got_norm:
+        x.wait()
+    gains[c, z, 0:1, 0:80] = (nt_v[...] + ns_v[...]).reshape(1, 80)
+
     ahead = [z > 0, z == N - 1, c >= 2, c >= N - 2, odd == 0]
     ahead = sum(x.astype(jnp.int32) for x in ahead)
     pl.when(ahead > 0)(lambda: pl.semaphore_wait(barrier, ahead))
@@ -165,7 +169,7 @@
         )
 
     def norm_step(k):
-        hop = {2: 1, 3: 2, 5: 3}.get(k)
+        hop = {2: 1, 3: 2, 4: 3}.get(k)
         for d in range(2):
             if hop is not None and hop < 4 - d:
                 gain_copy(d, hop - 1, 1).wait_recv()
@@ -201,48 +205,39 @@
 
     def begin(d):
         greet(d)
+        gain_copy(d, 0).start()
         piece_copy(d, 0).start()
 
-    def more(d):
-        gain_copy(d, 0).start()
-        piece_copy(d, 1).start()
-
-    def share_norm():
-        for x in got_norm:
-            x.wait()
-        gains[c, z, 0:1, 0:80] = (nt_v[...] + ns_v[...]).reshape(1, 80)
+    def second(*ways):
+        for d in ways:
+            piece_copy(d, 1).start()
 
     @pl.when(z == 0)
     def _():
         begin(0)
-        share_norm()
         for i in (5, 1, 4, 2, 3):
             compute(i)
-        more(0)
+        second(0)
         begin(1)
-        more(1)
+        second(1)
 
     @pl.when(z == N - 1)
     def _():
         begin(0)
         compute(5)
         begin(1)
-        share_norm()
         for i in (1, 4, 2, 3):
             compute(i)
-        more(0)
-        more(1)
+        second(0, 1)
 
     @pl.when(jnp.logical_not(rightmost))
     def _():
         begin(1)
         compute(5)
         begin(0)
-        share_norm()
         for i in (1, 4, 2, 3):
             compute(i)
-        more(1)
-        more(0)
+        second(1, 0)
 
     def item(k, met):
         for d in (1, 0):
@@ -266,7 +261,6 @@
     for k in range(DEPTH, low):
         norm_step(k)
         item(k, met)
-    norm_end()
     for parity in range(2):
 
         @pl.when(odd == parity)
@@ -274,6 +268,10 @@
             mine = set(met)
             for k in range(low, FIRST[parity]):
                 item(k, mine)
+                if k == low:
+                    norm_end()
+            if FIRST[parity] == low:
+                norm_end()
             drain(FIRST[parity], mine)
 
 
@@ -329,7 +327,7 @@
 
 
 def early(parity):
-    return (0, 1, -1, 2, -2) if FIRST[parity] == 7 else (0, 1, -1, 2, -2, 3, -3)
+    return (0, 1, -1, 2, -2) if FIRST[parity] == 5 else (0, 1, -1, 2, -2, 3, -3)
 
 
 def deliver(buf, gain, q, k, v, g, sem):

time: 95.9 us -> 95.9 us (level)
  no operation moved by 1% of the time
where the time goes in v5:
time: 95.9 us; the launch traced here: 95.8 us
  Pallas kernels  95.1 us (99%)
    pallas_call x1, Pallas kernels, local(): pl.pallas_call(exchange, name='exchange', out_shape=(jax.ShapeDtypeStruct...  75.5 us
    pallas_call x1, Pallas kernels, local(): pl.pallas_call(finish, name='finish', out_shape=jax.ShapeDtypeStruct((3,...  14.4 us
    pallas_call x1, Pallas kernels, local(): pl.pallas_call(deliver, name='deliver', out_shape=(*wide, jax.ShapeDtypeS...  4.05 us

profile of v5, /device:TPU:24, one launch (start us, length us, event | category | flops | bytes accessed | tf_op | source)
XLA Modules:
  0.0 95.8 jit_solution(219214104239885162)
XLA Ops:
  0.6 75.5 %exchange.1 = (bf16[8,896,640]{2,1,0:T(8,128)(2,1)S(1)}, f32[40,128]{1,0:T(8,128)S(1)}) custom-call(bf16[640,640]{1,0:T(8,128)(2,1)} %wq.1, bf16[32,640]{1,0:T(8,128)(2,1)} %bitcast.4, bf16[32,640]{1,0:T(8,128)(2,1)} %hq.1, bf16[640,128]{1,0:T(8,128)(2,1)} %wk.1, bf16[32,640]{1,0:T(8,128)(2,1)} %bitcast.5, bf16[32,128]{1,0:T(8,128)(2,1)} %hk.1, ...), custom_call_target="tpu_custom_call" | custom-call | tf_op jit(solution)/shard_map/exchange/pallas_call | solution.py:361
  76.2 4.0 %deliver.1 = (bf16[640,5120]{1,0:T(8,128)(2,1)}, bf16[128,5120]{1,0:T(8,128)(2,1)}, bf16[128,5120]{1,0:T(8,128)(2,1)}, bf16[40,128]{1,0:T(8,128)(2,1)}) custom-call(bf16[8,896,640]{2,1,0:T(8,128)(2,1)S(1)} %get-tuple-element.13.buf, f32[40,128]{1,0:T(8,128)S(1)} %get-tuple-element.14.gain), custom_call_target="tpu_custom_call" | custom-call | tf_op jit(solution)/shard_map/deliver/pallas_call | solution.py:395
  80.2 14.4 %finish.1.late = bf16[3,896,640]{2,1,0:T(8,128)(2,1)S(1)} custom-call(bf16[8,896,640]{2,1,0:T(8,128)(2,1)S(1)} %get-tuple-element.13.buf), custom_call_target="tpu_custom_call" | custom-call | tf_op jit(solution)/shard_map/finish/pallas_call | solution.py:404
  94.6 1.1 %deliver_late.1 = (bf16[640,5120]{1,0:T(8,128)(2,1)}, bf16[128,5120]{1,0:T(8,128)(2,1)}, bf16[128,5120]{1,0:T(8,128)(2,1)}) custom-call(bf16[3,896,640]{2,1,0:T(8,128)(2,1)S(1)} %finish.1.late, bf16[640,5120]{1,0:T(8,128)(2,1)} %get-tuple-element.15.q_in, ...), custom_call_target="tpu_custom_call", output_to_operand_aliasing={{0}: (1, {}), {1}: (2, {}), {2}: (3, {})} | custom-call | tf_op jit(solution)/shard_map/deliver_late/pallas_call | solution.py:413

commit v6 on v5

--- a/solution.py
+++ b/solution.py
@@ -22,10 +22,10 @@
     ((0, 128), (128, 320), (448, 448)),
     ((0, 448), (448, 448)),
     ((0, 448), (448, 448)),
-    ((0, 384), (384, 64)),
+    ((0, 368), (368, 80)),
 )
 RIGHT = [(h, *piece) for h, pieces in enumerate(HOPS) for piece in pieces]
-LEFT = [(h, WIDTH - first - height, height) for h, first, height in RIGHT[:-2]] + [(3, 448, 448), (3, 384, 64)]
+LEFT = [(h, WIDTH - first - height, height) for h, first, height in RIGHT[:-2]] + [(3, 448, 448), (3, 368, 80)]
 ORDERS = (RIGHT, LEFT)
 NS = len(RIGHT)
 LAST = NS - 1
@@ -34,8 +34,12 @@
 SIGN = (1, -1)
 
 
+def wrapped(x):
+    return x + N * (x < 0).astype(jnp.int32) - N * (x >= N).astype(jnp.int32)
+
+
 def source(z, d, steps):
-    return lax.rem(z - SIGN[d] * steps + N, N)
+    return wrapped(z - SIGN[d] * steps)
 
 
 def rows_of(d, k):
@@ -70,23 +74,6 @@
     wq_v, wk_v, wv_v, lq_v, lk_v, lv_v, hq_v, hk_v, hv_v, nt_v, ns_v, gains,
     in_sem, send_sem, recv_sem, gsend, grecv, psend, precv, ready,
 ):
-    z = lax.axis_index("rows")
-    c = lax.axis_index("cols")
-    to = (lax.rem(z + 1, N), lax.rem(z + N - 1, N))
-    up, down = lax.rem(c + 2, N), lax.rem(c + N - 2, N)
-    odd = lax.rem(c, 2)
-    partner = c + 1 - 2 * odd
-    barrier = pltpu.get_barrier_semaphore()
-
-    def signal(sem, **who):
-        pl.semaphore_signal(sem, inc=1, device_id=who, device_id_type=MESH)
-
-    pl.when(z < N - 1)(lambda: signal(barrier, rows=to[0]))
-    pl.when(z == 0)(lambda: signal(barrier, rows=to[1]))
-    pl.when(c < N - 2)(lambda: signal(barrier, cols=up))
-    pl.when(c < 2)(lambda: signal(barrier, cols=down))
-    pl.when(odd == 1)(lambda: signal(barrier, cols=partner))
-
     count = [0]
 
     def load(src, dst):
@@ -102,8 +89,25 @@
     for i in (1, 4, 2, 3):
         got[i] = [load(wq.at[:, pl.ds(i * UNIT, UNIT)], wq_v.at[i])]
 
+    z = lax.axis_index("rows")
+    c = lax.axis_index("cols")
+    to = (wrapped(z + 1), wrapped(z - 1))
+    up, down = wrapped(c + 2), wrapped(c - 2)
+    odd = lax.rem(c, 2)
+    partner = c + 1 - 2 * odd
+    barrier = pltpu.get_barrier_semaphore()
+
+    def signal(sem, **who):
+        pl.semaphore_signal(sem, inc=1, device_id=who, device_id_type=MESH)
+
+    pl.when(z < N - 2)(lambda: signal(barrier, rows=to[0]))
+    pl.when((z == 0) | (z == N - 1))(lambda: signal(barrier, rows=to[1]))
+    pl.when(c < N - 2)(lambda: signal(barrier, cols=up))
+    pl.when(c < 2)(lambda: signal(barrier, cols=down))
+    pl.when(odd == 1)(lambda: signal(barrier, cols=partner))
+
     def greet(d):
-        pl.when(z < N - 1 if d == 0 else z == 0)(lambda: pl.semaphore_wait(ready.at[d], 1))
+        pl.when(z < N - 2 if d == 0 else rightmost)(lambda: pl.semaphore_wait(ready.at[d], 1))
 
     def compute(i):
         for x in got[i]:
@@ -116,6 +120,14 @@
         delta = lax.dot_general(h, lt, (((0,), (0,)), ((), ())), preferred_element_type=F32)
         buf[z, pl.ds(i * UNIT, UNIT), :] = (w.T.astype(F32) + MIX * delta).astype(BF16)
 
+    ahead = [(z > 0) & (z < N - 1), z >= N - 2, c >= 2, c >= N - 2, odd == 0]
+    ahead = sum(x.astype(jnp.int32) for x in ahead)
+    pl.when(ahead > 0)(lambda: pl.semaphore_wait(barrier, ahead))
+    pl.when((z > 0) & (z < N - 1))(lambda: signal(ready.at[0], rows=to[1]))
+    pl.when(z >= N - 2)(lambda: signal(ready.at[1], rows=to[0]))
+    pl.when(c >= 2)(lambda: signal(ready.at[2], cols=down))
+    pl.when(odd == 0)(lambda: signal(ready.at[3], cols=partner))
+
     rightmost = (z == 0) | (z == N - 1)
 
     @pl.when(rightmost)
@@ -131,14 +143,6 @@
     for x in got_norm:
         x.wait()
     gains[c, z, 0:1, 0:80] = (nt_v[...] + ns_v[...]).reshape(1, 80)
-
-    ahead = [z > 0, z == N - 1, c >= 2, c >= N - 2, odd == 0]
-    ahead = sum(x.astype(jnp.int32) for x in ahead)
-    pl.when(ahead > 0)(lambda: pl.semaphore_wait(barrier, ahead))
-    pl.when(z > 0)(lambda: signal(ready.at[0], rows=to[1]))
-    pl.when(z == N - 1)(lambda: signal(ready.at[1], rows=to[0]))
-    pl.when(c >= 2)(lambda: signal(ready.at[2], cols=down))
-    pl.when(odd == 0)(lambda: signal(ready.at[3], cols=partner))
 
     def piece_copy(d, k, steps_more=0):
         ref = buf.at[source(z, d, ORDERS[d][k][0] + steps_more), rows_of(d, k), :]
@@ -162,7 +166,7 @@
         )
 
     def pair_copy(hop, steps_more=0):
-        ref = gains.at[pl.ds(lax.rem(c - odd - 2 * (hop + steps_more) + N, N), 2)]
+        ref = gains.at[pl.ds(wrapped(c - odd - 2 * (hop + steps_more)), 2)]
         return pltpu.make_async_remote_copy(
             src_ref=ref, dst_ref=ref, send_sem=psend.at[1 + hop], recv_sem=precv.at[1 + hop],
             device_id={"cols": up}, device_id_type=MESH,
@@ -278,7 +282,7 @@
 def finish(buf, late, send_sem, recv_sem):
     z = lax.axis_index("rows")
     odd = lax.rem(lax.axis_index("cols"), 2)
-    to = (lax.rem(z + 1, N), lax.rem(z + N - 1, N))
+    to = (wrapped(z + 1), wrapped(z - 1))
     barrier = pltpu.get_barrier_semaphore()
     for d in range(2):
         pl.semaphore_signal(barrier, inc=1, device_id={"rows": to[d]}, device_id_type=MESH)
@@ -315,7 +319,7 @@
 def write_out(outs, z, sem, blocks):
     copies = []
     for block, distance in blocks:
-        at = pl.ds(pl.multiple_of(lax.rem(z + distance + N, N) * ROWS, ROWS), ROWS)
+        at = pl.ds(pl.multiple_of(wrapped(z + distance) * ROWS, ROWS), ROWS)
         first = 0
         for out, width in zip(outs, COLS):
             copies.append(pltpu.make_async_copy(block.at[pl.ds(first, width), :], out.at[:, at], sem.at[len(copies)]))
@@ -338,7 +342,7 @@
 
         @pl.when(odd == parity)
         def _():
-            write_out((q, k, v), z, sem, [(buf.at[lax.rem(z + b + N, N)], b) for b in early(parity)])
+            write_out((q, k, v), z, sem, [(buf.at[wrapped(z + b)], b) for b in early(parity)])
 
 
 def deliver_late(late, q_in, k_in, v_in, q, k, v, sem):

time: 95.9 us -> 94.8 us (0.989)
  Pallas kernels: 95.1 us -> 94 us
    pallas_call x1, Pallas kernels: 14.4 us -> 13.4 us  [local(): pl.pallas_call(finish, name='finish', out_shape=jax.ShapeDtypeStruct((3,...]
where the time goes in v6:
time: 94.8 us; the launch traced here: 94.6 us
  Pallas kernels  94 us (99%)
    pallas_call x1, Pallas kernels, local(): pl.pallas_call(exchange, name='exchange', out_shape=(jax.ShapeDtypeStruct...  75.4 us
    pallas_call x1, Pallas kernels, local(): pl.pallas_call(finish, name='finish', out_shape=jax.ShapeDtypeStruct((3,...  13.4 us
    pallas_call x1, Pallas kernels, local(): pl.pallas_call(deliver, name='deliver', out_shape=(*wide, jax.ShapeDtypeS...  4.05 us

profile of v6, /device:TPU:24, one launch (start us, length us, event | category | flops | bytes accessed | tf_op | source)
XLA Modules:
  0.0 94.6 jit_solution(8106763680648429110)
XLA Ops:
  0.6 75.4 %exchange.1 = (bf16[8,896,640]{2,1,0:T(8,128)(2,1)S(1)}, f32[40,128]{1,0:T(8,128)S(1)}) custom-call(bf16[640,640]{1,0:T(8,128)(2,1)} %wq.1, bf16[32,640]{1,0:T(8,128)(2,1)} %bitcast.4, bf16[32,640]{1,0:T(8,128)(2,1)} %hq.1, bf16[640,128]{1,0:T(8,128)(2,1)} %wk.1, bf16[32,640]{1,0:T(8,128)(2,1)} %bitcast.5, bf16[32,128]{1,0:T(8,128)(2,1)} %hk.1, ...), custom_call_target="tpu_custom_call" | custom-call | tf_op jit(solution)/shard_map/exchange/pallas_call | solution.py:365
  76.1 4.1 %deliver.1 = (bf16[640,5120]{1,0:T(8,128)(2,1)}, bf16[128,5120]{1,0:T(8,128)(2,1)}, bf16[128,5120]{1,0:T(8,128)(2,1)}, bf16[40,128]{1,0:T(8,128)(2,1)}) custom-call(bf16[8,896,640]{2,1,0:T(8,128)(2,1)S(1)} %get-tuple-element.13.buf, f32[40,128]{1,0:T(8,128)S(1)} %get-tuple-element.14.gain), custom_call_target="tpu_custom_call" | custom-call | tf_op jit(solution)/shard_map/deliver/pallas_call | solution.py:399
  80.1 13.4 %finish.1.late = bf16[3,896,640]{2,1,0:T(8,128)(2,1)S(1)} custom-call(bf16[8,896,640]{2,1,0:T(8,128)(2,1)S(1)} %get-tuple-element.13.buf), custom_call_target="tpu_custom_call" | custom-call | tf_op jit(solution)/shard_map/finish/pallas_call | solution.py:408
  93.5 1.2 %deliver_late.1 = (bf16[640,5120]{1,0:T(8,128)(2,1)}, bf16[128,5120]{1,0:T(8,128)(2,1)}, bf16[128,5120]{1,0:T(8,128)(2,1)}) custom-call(bf16[3,896,640]{2,1,0:T(8,128)(2,1)S(1)} %finish.1.late, bf16[640,5120]{1,0:T(8,128)(2,1)} %get-tuple-element.15.q_in, ...), custom_call_target="tpu_custom_call", output_to_operand_aliasing={{0}: (1, {}), {1}: (2, {}), {2}: (3, {})} | custom-call | tf_op jit(solution)/shard_map/deliver_late/pallas_call | solution.py:417

commit v7 on v6

--- a/solution.py
+++ b/solution.py
@@ -288,13 +288,23 @@
         pl.semaphore_signal(barrier, inc=1, device_id={"rows": to[d]}, device_id_type=MESH)
     pl.semaphore_wait(barrier, 2)
 
+    low = min(FIRST)
+    rest = max(FIRST)
+
     def piece_copy(d, k, first):
         hop = ORDERS[d][k][0]
         here = late.at[d] if needs(d, k)[0] >= first else buf.at[source(z, d, hop)]
         return pltpu.make_async_remote_copy(
             src_ref=here.at[rows_of(d, k), :], dst_ref=late.at[2 if hop == 3 else d, rows_of(d, k), :],
-            send_sem=send_sem.at[d, k], recv_sem=recv_sem.at[d, k],
+            send_sem=send_sem.at[0 if k < rest else 1 if k < LAST else 2 + d],
+            recv_sem=recv_sem.at[2 * (k - low) + d if k < rest else 2 * (rest - low)],
             device_id={"rows": to[d]}, device_id_type=MESH,
+        )
+
+    def of_size(ref, send, recv):
+        return pltpu.make_async_remote_copy(
+            src_ref=ref, dst_ref=ref, send_sem=send_sem.at[send], recv_sem=recv_sem.at[recv],
+            device_id={"rows": to[0]}, device_id_type=MESH,
         )
 
     for parity, first in enumerate(FIRST):
@@ -309,25 +319,29 @@
                             piece_copy(d, i, first).wait_recv()
                             met.add((d, i))
                     if_sent(z, d, k, lambda d=d, k=k: piece_copy(d, k, first).start())
-            for k in range(first, NS):
-                for d in (1, 0):
-                    if_sent(z, d, k, lambda d=d, k=k: piece_copy(d, k, first).wait_send())
+            for k in range(first, rest):
+                for d in range(2):
                     if (d, k) not in met:
-                        if_received(z, d, k, lambda d=d, k=k: piece_copy(d, k, first).wait_recv())
-
-
-def write_out(outs, z, sem, blocks):
-    copies = []
-    for block, distance in blocks:
+                        piece_copy(d, k, first).wait_recv()
+            if first < rest:
+                of_size(late.at[pl.ds(0, 2)], 0, 0).wait_send()
+            sent = sum(ORDERS[d][rest][2] for d in range(2))
+            of_size(late.at[2, pl.ds(0, sent), :], 1, 0).wait_send()
+            for d in range(2):
+                if_sent(z, d, LAST, lambda d=d: piece_copy(d, LAST, first).wait_send())
+            of_size(late.at[2], 0, 2 * (rest - low)).wait_recv()
+
+
+def write_out(outs, z, sem, blocks_of, blocks):
+    for index, distance in blocks:
+        block = blocks_of.at[index]
         at = pl.ds(pl.multiple_of(wrapped(z + distance) * ROWS, ROWS), ROWS)
         first = 0
         for out, width in zip(outs, COLS):
-            copies.append(pltpu.make_async_copy(block.at[pl.ds(first, width), :], out.at[:, at], sem.at[len(copies)]))
+            pltpu.make_async_copy(block.at[pl.ds(first, width), :], out.at[:, at], sem.at[0]).start()
             first += width
-    for copy in copies:
-        copy.start()
-    for copy in copies:
-        copy.wait()
+    everything = blocks_of.at[pl.ds(0, len(blocks))]
+    pltpu.make_async_copy(everything, everything, sem.at[0]).wait()
 
 
 def early(parity):
@@ -342,7 +356,7 @@
 
         @pl.when(odd == parity)
         def _():
-            write_out((q, k, v), z, sem, [(buf.at[wrapped(z + b)], b) for b in early(parity)])
+            write_out((q, k, v), z, sem, buf, [(wrapped(z + b), b) for b in early(parity)])
 
 
 def deliver_late(late, q_in, k_in, v_in, q, k, v, sem):
@@ -352,8 +366,7 @@
 
         @pl.when(odd == parity)
         def _():
-            blocks = [(late.at[slot], b) for slot, b in enumerate((-3, 3, 4)) if b not in early(parity)]
-            write_out((q, k, v), z, sem, blocks)
+            write_out((q, k, v), z, sem, late, [(slot, b) for slot, b in enumerate((-3, 3, 4)) if b not in early(parity)])
 
 
 def local(wq, lq, hq, wk, lk, hk, wv, lv, hv, nt, ns):
@@ -402,7 +415,7 @@
         out_shape=(*wide, jax.ShapeDtypeStruct((40, PAD), BF16)),
         in_specs=[vmem, vmem],
         out_specs=(hbm, hbm, hbm, vmem),
-        scratch_shapes=[dma((32,))],
+        scratch_shapes=[dma((1,))],
         compiler_params=pltpu.CompilerParams(vmem_limit_bytes=limit, has_side_effects=True),
     )(buf, gain)
     late = pl.pallas_call(
@@ -411,7 +424,7 @@
         out_shape=jax.ShapeDtypeStruct((3, WIDTH, ROWS), BF16),
         in_specs=[vmem],
         out_specs=vmem,
-        scratch_shapes=[dma((2, NS)), dma((2, NS))],
+        scratch_shapes=[dma((4,)), dma((2 * (max(FIRST) - min(FIRST)) + 1,))],
         compiler_params=pltpu.CompilerParams(collective_id=1, has_side_effects=True, vmem_limit_bytes=limit),
     )(buf)
     q, k, v = pl.pallas_call(
@@ -420,7 +433,7 @@
         out_shape=tuple(wide),
         in_specs=[vmem, hbm, hbm, hbm],
         out_specs=(hbm, hbm, hbm),
-        scratch_shapes=[dma((16,))],
+        scratch_shapes=[dma((1,))],
         input_output_aliases={1: 0, 2: 1, 3: 2},
         compiler_params=pltpu.CompilerParams(vmem_limit_bytes=limit),
     )(late, q, k, v)

time: 94.8 us -> 94.4 us (level)
  no operation moved by 1% of the time
where the time goes in v7:
time: 94.4 us; the launch traced here: 94.3 us
  Pallas kernels  93.6 us (99%)
    pallas_call x1, Pallas kernels, local(): pl.pallas_call(exchange, name='exchange', out_shape=(jax.ShapeDtypeStruct...  75.7 us
    pallas_call x1, Pallas kernels, local(): pl.pallas_call(finish, name='finish', out_shape=jax.ShapeDtypeStruct((3,...  13.1 us
    pallas_call x1, Pallas kernels, local(): pl.pallas_call(deliver, name='deliver', out_shape=(*wide, jax.ShapeDtypeS...  3.77 us

profile of v7, /device:TPU:24, one launch (start us, length us, event | category | flops | bytes accessed | tf_op | source)
XLA Modules:
  0.0 94.3 jit_solution(13840064758324532177)
XLA Ops:
  0.6 75.7 %exchange.1 = (bf16[8,896,640]{2,1,0:T(8,128)(2,1)S(1)}, f32[40,128]{1,0:T(8,128)S(1)}) custom-call(bf16[640,640]{1,0:T(8,128)(2,1)} %wq.1, bf16[32,640]{1,0:T(8,128)(2,1)} %bitcast.4, bf16[32,640]{1,0:T(8,128)(2,1)} %hq.1, bf16[640,128]{1,0:T(8,128)(2,1)} %wk.1, bf16[32,640]{1,0:T(8,128)(2,1)} %bitcast.5, bf16[32,128]{1,0:T(8,128)(2,1)} %hk.1, ...), custom_call_target="tpu_custom_call" | custom-call | tf_op jit(solution)/shard_map/exchange/pallas_call | solution.py:378
  76.3 3.8 %deliver.1 = (bf16[640,5120]{1,0:T(8,128)(2,1)}, bf16[128,5120]{1,0:T(8,128)(2,1)}, bf16[128,5120]{1,0:T(8,128)(2,1)}, bf16[40,128]{1,0:T(8,128)(2,1)}) custom-call(bf16[8,896,640]{2,1,0:T(8,128)(2,1)S(1)} %get-tuple-element.13.buf, f32[40,128]{1,0:T(8,128)S(1)} %get-tuple-element.14.gain), custom_call_target="tpu_custom_call" | custom-call | tf_op jit(solution)/shard_map/deliver/pallas_call | solution.py:412
  80.1 13.1 %finish.1.late = bf16[3,896,640]{2,1,0:T(8,128)(2,1)S(1)} custom-call(bf16[8,896,640]{2,1,0:T(8,128)(2,1)S(1)} %get-tuple-element.13.buf), custom_call_target="tpu_custom_call" | custom-call | tf_op jit(solution)/shard_map/finish/pallas_call | solution.py:421
  93.3 1.0 %deliver_late.1 = (bf16[640,5120]{1,0:T(8,128)(2,1)}, bf16[128,5120]{1,0:T(8,128)(2,1)}, bf16[128,5120]{1,0:T(8,128)(2,1)}) custom-call(bf16[3,896,640]{2,1,0:T(8,128)(2,1)S(1)} %finish.1.late, bf16[640,5120]{1,0:T(8,128)(2,1)} %get-tuple-element.15.q_in, ...), custom_call_target="tpu_custom_call", output_to_operand_aliasing={{0}: (1, {}), {1}: (2, {}), {2}: (3, {})} | custom-call | tf_op jit(solution)/shard_map/deliver_late/pallas_call | solution.py:430
